TPU v7x, 256 devices: a whole 4x4x8 slice. The times are simulated.
256 devices in a mesh: seq: 16 (over z, core), head: 16 (over x, y).
Axes of the slice: x: 4, y: 4, z: 8, core: 2. Of those that a mesh axis runs over, the one named last changes fastest.
Arguments:
- tokens: bfloat16 [2048, 4096], P('seq', 'head'), may hold values from -6 to 6
- w_query: bfloat16 [4096, 4096], P(None, 'head'), may hold values from -0.09375 to 0.09375
- w_key: bfloat16 [4096, 4096], P(None, 'head'), may hold values from -0.09375 to 0.09375
- w_value: bfloat16 [4096, 4096], P(None, 'head'), may hold values from -0.09375 to 0.09375
- upstream: bfloat16 [2048, 4096], P('seq', 'head'), may hold values from -6 to 6
- log_decay: float32 [2048, 32], P('seq', 'head'), may hold values from -1 to 0, as said below
- segment: int32 [2048], replicated, may hold values from 0 to 7, never falling along the last dimension, each value on 1 to 512 neighbouring positions
Outputs:
- grad_query: bfloat16 [4096, 4096], P('seq', 'head')
- grad_key: bfloat16 [4096, 4096], P('seq', 'head')
- grad_value: bfloat16 [4096, 4096], P('seq', 'head')
Inputs may be any that keep to these rules, and one draw needn't show every extreme that they name: log_decay is negative. `segment`: document ids never fall along the tokens; each document holds 1 to 512 tokens.
All inputs are finite; a program needn't handle non-finite values.
Results may differ from a plain program's by a relative error of at most 0.02.
Values may be sent and summed in bfloat16 or wider, within the bound.
A program may use at most 64 MiB of HBM per device.

v0:
```python
import jax
import jax.numpy as jnp
from jax import lax
from jax.sharding import Mesh
from jax.sharding import PartitionSpec as P

HEAD = 128
SEQ = ("seq_0", "seq_1")


def copy_for_each(x, axis):
    count = lax.axis_size(axis)
    return lax.all_to_all(jnp.broadcast_to(x[None], (count, *x.shape)), axis, 0, 0, tiled=True)


def joined_along(parts, dim):
    dims = list(parts.shape[1:])
    dims[dim] *= parts.shape[0]
    return jnp.moveaxis(parts, 0, dim).reshape(dims)


def collect(x, axis, dim):
    parts = copy_for_each(x, axis)
    return joined_along(parts, dim)


def filled_with(x, identity):
    return jax.tree.map(
        lambda part, zero: jnp.zeros_like(part) + jnp.asarray(zero, part.dtype), x, identity
    )


def prefix_by_axis(x, axes, combine, identity, reverse):
    before = start = filled_with(x, identity)
    so_far = x
    for axis in reversed(axes):
        count, place = (lax.axis_size(axis), lax.axis_index(axis))
        pieces = jax.tree.map(
            lambda part, kind: lax.all_gather(part.astype(kind), axis),
            so_far,
            (jnp.bfloat16, jnp.bfloat16),
        )
        inside, so_far = (start, start)
        for k in reversed(range(count)) if reverse else range(count):
            passed = k > place if reverse else k < place
            so_far = combine(
                so_far, jax.tree.map(lambda part, own: part[k].astype(own.dtype), pieces, x)
            )
            inside = jax.tree.map(lambda new, old: jnp.where(passed, new, old), so_far, inside)
        before = combine(inside, before)
    return before


def block_factors(log_rates, segs, previous):
    log_sum = jnp.cumsum(log_rates, axis=0)
    last_sum = log_sum[-1]
    last_seg = segs[-1]
    state_entering = jnp.where((segs == previous)[:, None], jnp.exp(log_sum), 0.0)
    state_leaving = jnp.where(
        (segs == last_seg)[:, None], jnp.exp(last_sum[None, :] - log_sum), 0.0
    )
    carry_decay = jnp.where(last_seg == previous, jnp.exp(last_sum), 0.0)
    places = jnp.arange(segs.shape[0], dtype=jnp.int32)
    same = (segs[:, None] == segs[None, :]) & (places[:, None] >= places[None, :])
    spread = log_sum.T[:, :, None] - log_sum.T[:, None, :]
    decay_mat = jnp.where(
        same[None], HEAD ** (-0.5) * jnp.exp(jnp.where(same[None], spread, 0.0)), 0.0
    )
    return (state_entering, state_leaving, carry_decay, decay_mat)


def combine(earlier, later):
    return (earlier[0] * later[0], later[0][:, None, None] * earlier[1] + later[1])


def local(tokens, w_query, w_key, w_value, upstream, log_decay, segment):
    rows = tokens.shape[0]
    width = w_query.shape[1]
    heads = width // HEAD
    piece = collect(tokens, "head", 1)

    def partial_product(weight):
        return jnp.dot(piece, weight, preferred_element_type=jnp.float32)

    query_sum = partial_product(w_query)
    key_sum = partial_product(w_key)
    value_sum = partial_product(w_value)
    query = query_sum.astype(jnp.bfloat16).reshape(rows, heads, HEAD)
    key_rows = key_sum.astype(jnp.bfloat16).reshape(rows, heads, HEAD)
    value_rows = value_sum.astype(jnp.bfloat16).reshape(rows, heads, HEAD)
    output_gradient = upstream.reshape(rows, heads, HEAD)
    my_index = lax.axis_index(SEQ)
    first = my_index * rows
    segs = lax.dynamic_slice_in_dim(segment, first, rows)
    before = lax.dynamic_slice_in_dim(segment, jnp.maximum(first - 1, 0), 1)[0]
    previous = jnp.where(my_index > 0, before, jnp.int32(-1))
    state_entering, state_leaving, carry_decay, decay_mat = block_factors(log_decay, segs, previous)
    scale = HEAD ** (-0.5)
    weighted_keys = (scale * state_leaving[:, :, None] * key_rows).astype(jnp.bfloat16)
    segment_state = jnp.einsum(
        "bdw,bdq->dwq", weighted_keys, value_rows, preferred_element_type=jnp.float32
    )
    weighted_queries = (scale * state_entering[:, :, None] * query).astype(jnp.bfloat16)
    following_state = jnp.einsum(
        "bdw,bdq->dwq", weighted_queries, output_gradient, preferred_element_type=jnp.float32
    )
    identity = (jnp.ones_like(carry_decay), jnp.zeros_like(segment_state))
    arriving_state = prefix_by_axis((carry_decay, segment_state), SEQ, combine, identity, False)[1]
    backward_state = prefix_by_axis((carry_decay, following_state), SEQ, combine, identity, True)[1]
    upper_limit = lax.Precision.HIGHEST
    score_qk = jnp.einsum("thd,shd->hts", query, key_rows, preferred_element_type=jnp.float32)
    attention_query_key = (decay_mat * score_qk).astype(jnp.bfloat16)
    score_up = jnp.einsum(
        "thd,shd->hts", output_gradient, value_rows, preferred_element_type=jnp.float32
    )
    attention_upstream = (decay_mat * score_up).astype(jnp.bfloat16)
    output_gradient_float = output_gradient.astype(jnp.float32)
    query_gradient = jnp.einsum(
        "wcz,zwm->cwm", attention_upstream, key_rows, preferred_element_type=jnp.float32
    ) + state_entering[:, :, None] * jnp.einsum(
        "pzo,zao->pza", output_gradient_float, arriving_state, precision=upper_limit
    )
    key_gradient = jnp.einsum(
        "voi,ovw->ivw", attention_upstream, query, preferred_element_type=jnp.float32
    ) + state_leaving[:, :, None] * jnp.einsum(
        "ixz,xqz->ixq", value_rows.astype(jnp.float32), backward_state, precision=upper_limit
    )
    value_gradient = jnp.einsum(
        "voi,ovw->ivw", attention_query_key, output_gradient, preferred_element_type=jnp.float32
    ) + state_leaving[:, :, None] * jnp.einsum(
        "dqg,qgf->dqf", key_rows.astype(jnp.float32), backward_state, precision=upper_limit
    )
    grads = jnp.concatenate(
        [
            query_gradient.astype(jnp.bfloat16).reshape(rows, width),
            key_gradient.astype(jnp.bfloat16).reshape(rows, width),
            value_gradient.astype(jnp.bfloat16).reshape(rows, width),
        ],
        axis=1,
    )
    contract = (((0,), (0,)), ((), ()))
    columns = lax.all_to_all(piece, SEQ, split_axis=1, concat_axis=0, tiled=True)
    every = lax.all_gather(grads, SEQ, axis=0, tiled=True)
    sums = lax.dot_general(columns, every, contract, preferred_element_type=jnp.float32)
    grad_query = sums[:, :width].astype(jnp.bfloat16)
    grad_key = sums[:, width : 2 * width].astype(jnp.bfloat16)
    grad_value = sums[:, 2 * width :].astype(jnp.bfloat16)
    return (grad_query, grad_key, grad_value)


def solution(mesh):
    torus = Mesh(mesh.devices.reshape(8, 2, mesh.shape["head"]), ("seq_0", "seq_1", "head"))
    in_specs = (
        P(SEQ, "head"),
        P(None, "head"),
        P(None, "head"),
        P(None, "head"),
        P(SEQ, "head"),
        P(SEQ, "head"),
        P(),
    )
    out_specs = (P(SEQ, "head"), P(SEQ, "head"), P(SEQ, "head"))
    return jax.shard_map(local, mesh=torus, in_specs=in_specs, out_specs=out_specs, check_vma=False)
```

profile of v0, /device:TPU:1, one launch (start us, length us, event | category | flops | bytes accessed | tf_op | source)
XLA Modules:
  0.0 220.8 jit_solution(14004489600486633102)
XLA Ops:
  9.5 7.6 %all-to-all-start = ((bf16[16,128,256]{1,2,0:T(8,128)(2,1)}), bf16[16,128,256]{1,2,0:T(8,128)(2,1)S(1)}, u32[]{:S(2)}, u32[]{:S(2)}) async-start(bf16[16,128,256]{1,2,0:T(8,128)(2,1)} %broadcast_in_dim.42), calls=%async_computation | async-start | bytes 2097152 | tf_op jit(solution)/shard_map/all_to_all | solution.py:13
  21.4 2.4 %all-gather.2 = bf16[2,1,2]{2,1,0:T(2,128)(2,1)S(1)} all-gather(bf16[1,1,2]{2,1,0:T(2,128)(2,1)S(1)} %get-tuple-element.48), channel_id=1, replica_groups=mesh['seq_0'=8,'seq_1'=2,'head'=16] {'seq_1'}, dimensions={0}, use_global_device_ids=true | all-gather | bytes 12 | tf_op jit(solution)/shard_map/all_gather | solution.py:39
  24.4 16.0 %all-gather.3 = bf16[8,1,2]{2,1,0:T(2,128)(2,1)S(1)} all-gather(bf16[1,1,2]{2,1,0:T(2,128)(2,1)S(1)} %multiply_convert_fusion.4), channel_id=1, replica_groups=mesh['seq_0'=8,'seq_1'=2,'head'=16] {'seq_0'}, dimensions={0}, use_global_device_ids=true | all-gather | bytes 36 | tf_op jit(solution)/shard_map/all_gather | solution.py:39
  48.6 5.1 %all-gather.1 = bf16[4,128,128]{2,1,0:T(8,128)(2,1)S(1)} all-gather(bf16[2,128,128]{2,1,0:T(8,128)(2,1)S(1)} %convolution_convert_fusion.4), channel_id=3, replica_groups=mesh['seq_0'=8,'seq_1'=2,'head'=16] {'seq_1'}, dimensions={0}, use_global_device_ids=true | all-gather | bytes 196608 | tf_op jit(solution)/shard_map/all_gather | solution.py:39
  56.3 19.2 %all_gather.42 = bf16[8,2,128,128]{3,2,1,0:T(8,128)(2,1)S(1)} all-gather(bf16[1,2,128,128]{3,2,1,0:T(8,128)(2,1)S(1)} %copy.188), channel_id=1, replica_groups=mesh['seq_0'=8,'seq_1'=2,'head'=16] {'seq_0'}, dimensions={0}, use_global_device_ids=true | all-gather | bytes 589824 | tf_op jit(solution)/shard_map/all_gather | solution.py:39
  76.3 1.6 copy.227
  79.4 1.6 copy.232
  81.0 1.6 copy.231
  84.1 1.6 copy.229
  92.7 8.1 %all-gather = bf16[4,128,128]{2,1,0:T(8,128)(2,1)S(1)} all-gather(bf16[2,128,128]{2,1,0:T(8,128)(2,1)S(1)} %convolution_convert_fusion.5), channel_id=2, replica_groups=mesh['seq_0'=8,'seq_1'=2,'head'=16] {'seq_1'}, dimensions={0}, use_global_device_ids=true | all-gather | bytes 196608 | tf_op jit(solution)/shard_map/all_gather | solution.py:39
  102.4 1.6 copy.215
  103.9 1.6 fusion.26
  105.5 1.6 copy.171
  108.1 2.0 fusion.12
  110.1 19.5 %all_gather.39 = bf16[8,2,128,128]{3,2,1,0:T(8,128)(2,1)S(1)} all-gather(bf16[1,2,128,128]{3,2,1,0:T(8,128)(2,1)} %copy.171), channel_id=1, replica_groups=mesh['seq_0'=8,'seq_1'=2,'head'=16] {'seq_0'}, dimensions={0}, use_global_device_ids=true | all-gather | bytes 589824 | tf_op jit(solution)/shard_map/all_gather | solution.py:39
  130.3 1.6 copy.217
  131.9 1.6 copy.223
  133.4 1.6 copy.222
  139.7 1.6 copy.218
  141.3 1.6 copy.224
  143.1 1.7 fusion.5
  145.7 44.5 %all_to_all.21 = bf16[128,16,256]{0,2,1:T(8,128)(2,1)} all-to-all(bf16[128,16,256]{0,2,1:T(8,128)(2,1)S(1)} %bitcast.249), channel_id=1, replica_groups=mesh['seq_0'=8,'seq_1'=2,'head'=16] {'seq_0','seq_1'}, dimensions={1} | all-to-all | bytes 2097152 | tf_op jit(solution)/shard_map/all_to_all | solution.py:142
  191.7 17.1 %all-gather.6.cloned.1.call-done = bf16[2048,768]{0,1:T(8,128)(2,1)} async-done(((bf16[128,768]{0,1:T(8,128)(2,1)}), bf16[2048,768]{0,1:T(8,128)(2,1)}) %all-gather.6.cloned.1.call-update) | async-done | bytes 3145744 | tf_op jit(solution)/shard_map/all_gather | solution.py:143
  208.8 2.9 %fusion = bf16[256,768]{0,1:T(8,128)(2,1)S(1)} fusion(bf16[2048,768]{0,1:T(8,128)(2,1)} %all-gather.6.cloned.1.call-done, bf16[2048,256]{1,0:T(8,128)(2,1)S(1)} %bitcast.255), kind=kOutput, calls=%fused_computation.1 | convolution fusion | flops 805502976 | bytes 4587520 | tf_op jit(solution)/shard_map/dot_general | solution.py:144
  (83 shorter events, 40.4 us)
Async XLA Ops:
  7.2 37.3 %copy-start = (bf16[4096,256]{1,0:T(8,128)(2,1)S(1)}, bf16[4096,256]{1,0:T(8,128)(2,1)}, u32[]{:S(2)}) copy-start(bf16[4096,256]{1,0:T(8,128)(2,1)} %param.10) | copy-start | bytes 6291460
  7.2 13.9 %copy-start.12 = (f32[128,2]{0,1:T(2,128)S(1)}, f32[128,2]{0,1:T(2,128)}, u32[]{:S(2)}) copy-start(f32[128,2]{0,1:T(2,128)} %param.12) | copy-start | bytes 3076
  7.2 34.5 %copy-start.6 = (bf16[128,256]{1,0:T(8,128)(2,1)S(1)}, bf16[128,256]{1,0:T(8,128)(2,1)}, u32[]{:S(2)}) copy-start(bf16[128,256]{1,0:T(8,128)(2,1)} %param.11) | copy-start | bytes 196612
  9.5 34.9 %all-to-all-start = ((bf16[16,128,256]{1,2,0:T(8,128)(2,1)}), bf16[16,128,256]{1,2,0:T(8,128)(2,1)S(1)}, u32[]{:S(2)}, u32[]{:S(2)}) async-start(bf16[16,128,256]{1,2,0:T(8,128)(2,1)} %broadcast_in_dim.42), calls=%async_computation | async-start | bytes 2097152 | tf_op jit(solution)/shard_map/all_to_all | solution.py:13
  17.1 191.7 %all-gather.6.cloned.1.call-start = ((), (), s32[]{:S(2)}) async-start(), calls=%async_computation.2 | async-start | bytes 3342336 | tf_op jit(solution)/shard_map/all_gather | solution.py:143
  41.8 6.7 %copy-start.3 = (bf16[128,256]{0,1:T(8,128)(2,1)}, bf16[128,256]{0,1:T(8,128)(2,1)S(1)}, u32[]{:S(2)}) copy-start(bf16[128,256]{0,1:T(8,128)(2,1)S(1)} %copy.236) | copy-start | bytes 196612
  44.5 1.6 copy-start.1
  46.0 1.6 copy-start.2
  102.3 3.2 %copy-start.4 = (bf16[2,128,128]{1,2,0:T(8,128)(2,1)}, bf16[2,128,128]{1,2,0:T(8,128)(2,1)S(1)}, u32[]{:S(2)}) copy-start(bf16[2,128,128]{1,2,0:T(8,128)(2,1)S(1)} %copy.216) | copy-start | bytes 196612
  108.1 34.9 %copy-start.5 = (bf16[2,128,128]{1,2,0:T(8,128)(2,1)S(1)}, bf16[2,128,128]{1,2,0:T(8,128)(2,1)}, u32[]{:S(2)}) copy-start(bf16[2,128,128]{1,2,0:T(8,128)(2,1)} %copy-done.4) | copy-start | bytes 196612
  110.1 33.0 %copy-start.8 = (f32[2]{0:T(128)S(1)}, f32[2]{0:T(128)}, u32[]{:S(2)}) copy-start(f32[2]{0:T(128)} %get-tuple-element.60) | copy-start | bytes 28
  110.1 33.0 %copy-start.9 = (f32[2]{0:T(128)S(1)}, f32[2]{0:T(128)}, u32[]{:S(2)}) copy-start(f32[2]{0:T(128)} %get-tuple-element.63) | copy-start | bytes 28
  110.1 33.0 %copy-start.10 = (f32[2]{0:T(128)S(1)}, f32[2]{0:T(128)}, u32[]{:S(2)}) copy-start(f32[2]{0:T(128)} %get-tuple-element.50) | copy-start | bytes 28
  110.1 33.0 %copy-start.11 = (f32[2]{0:T(128)S(1)}, f32[2]{0:T(128)}, u32[]{:S(2)}) copy-start(f32[2]{0:T(128)} %get-tuple-element.51) | copy-start | bytes 28
  142.8 2.1 copy-start.7
Sparse Core Ops, SparseCore 0:
  145.8 62.9 all-gather.5
where the time goes:
time: 222 us; the launch traced here: 221 us
  blocking collectives  115 us (52%)
  local copies, waits for them, and re-layouts  42.9 us (19%)
  waiting for transfers between devices  17.1 us (8%)
  between operations  15.7 us (7%)
  matrix products  13 us (6%)
  other arithmetic  9.77 us (4%)
  starting transfers between devices  7.61 us (3%)
    all_gather x6, blocking collectives, prefix_by_axis(): lax.all_gather(part.astype(kind), axis)  70.2 us
    all_to_all x1, blocking collectives, local(): lax.all_to_all(piece, SEQ, split_axis=1, concat_axis=0, tiled=True)  44.5 us
    unnamed x51, local copies, waits for them, and re-layouts  32.5 us
    all_gather x1, waiting for transfers between devices, local(): every = lax.all_gather(grads, SEQ, axis=0, tiled=True)  17.1 us
    all_to_all x1, starting transfers between devices, copy_for_each(): lax.all_to_all(jnp.broadcast_to(x[None], (count, *x.shape)), axis, 0, 0,...  7.57 us
  transfers between devices with their start and end apart: 2, of which 1 were waited for; matrix products, arithmetic and copies ran while one was open for 4% of the time, Pallas kernels for 0%

commit v1 on v0

v1 whole, which is shorter than its diff:
```python
import functools

import jax
import jax.numpy as jnp
from jax import lax
from jax.experimental import pallas as pl
from jax.experimental.pallas import tpu as pltpu
from jax.sharding import PartitionSpec as P

HEAD = 128
SCALE = HEAD ** (-0.5)
MESH = pl.DeviceIdType.MESH
BF16, F32 = jnp.bfloat16, jnp.float32


def dot(a, b, da, db):
    return lax.dot_general(a, b, (((da,), (db,)), ((), ())), preferred_element_type=F32)


def kernel(
    tok, wq, wk, wv, up, ldt, segv, segs,
    out_q, out_k, out_v,
    x_all, w_all, qkv, qkv_x, upb, up_x, lsb, ct,
    gl, inm, outm, carry, lst, rst, inc, ret, grad, rows_x, rows_r,
    x_recv, x_send, c_recv, c_send, z_recv, z_send, l_recv, l_send, u_recv, u_send,
    g_recv, g_send, d_recv, d_send, o_recv, o_send, loc,
):
    seq, head = lax.axis_index("seq"), lax.axis_index("head")
    z, c = seq // 2, seq % 2
    x, y = head // 4, head % 4
    other = 1 - c

    def at(dz=None, core=None, hx=None, hy=None):
        zz = z if dz is None else dz
        cc = c if core is None else core
        xx = x if hx is None else hx
        yy = y if hy is None else hy
        return {"seq": zz * 2 + cc, "head": xx * 4 + yy}

    xs = [(x + i) % 4 for i in range(4)]
    ys = [(y + i) % 4 for i in range(4)]
    zs = [(z + i) % 8 for i in range(8)]
    partner = at(core=other)
    x_up, x_dn, y_up, y_dn = at(hx=xs[1]), at(hx=xs[3]), at(hy=ys[1]), at(hy=ys[3])
    z_up, z_dn = at(dz=zs[1]), at(dz=zs[7])

    sent = []

    def send(src, dst, ssem, rsem, dev):
        copy = pltpu.make_async_remote_copy(
            src_ref=src, dst_ref=dst, send_sem=ssem, recv_sem=rsem, device_id=dev, device_id_type=MESH
        )
        copy.start()
        sent.append(copy)

    def arrived(dst, ssem, rsem):
        pltpu.make_async_remote_copy(
            src_ref=dst, dst_ref=dst, send_sem=ssem, recv_sem=rsem, device_id=partner, device_id_type=MESH
        ).wait_recv()

    weights = []
    for i, w in enumerate((wq, wk, wv)):
        copy = pltpu.make_async_copy(w, w_all.at[i], loc.at[i])
        copy.start()
        weights.append(copy)
    own_tok = pltpu.make_async_copy(tok, x_all.at[head], loc.at[3])
    own_tok.start()
    own_up = pltpu.make_async_copy(up.at[:, pl.ds(pl.multiple_of(c * 128, 128), 128)], upb.at[seq], loc.at[4])
    own_up.start()
    oth_up = pltpu.make_async_copy(up.at[:, pl.ds(pl.multiple_of(other * 128, 128), 128)], up_x, loc.at[5])
    oth_up.start()

    barrier = pltpu.get_barrier_semaphore()
    near = (partner, x_up, x_dn, y_up, y_dn, z_up, z_dn)
    for dev in near:
        pl.semaphore_signal(barrier, inc=1, device_id=dev, device_id_type=MESH)

    total = jnp.concatenate([ldt[...], jnp.zeros((6, 128), F32)], axis=0)
    lane = lax.broadcasted_iota(jnp.int32, (8, 128), 1)
    for k in (1, 2, 4, 8, 16, 32, 64):
        total = total + jnp.where(lane >= k, pltpu.roll(total, k, 1), 0.0)
    lsb[seq] = total

    own_tok.wait()
    own_up.wait()
    oth_up.wait()
    pl.semaphore_wait(barrier, len(near))

    def plane(unit, recv, sends):
        count = [0]

        def push(ox, oy, half, sub, dev):
            h = ox * 4 + oy
            i = count[0]
            count[0] += 1
            view = unit(h, half, sub)
            send(view, view, sends.at[i], recv.at[half * 2 + (0 if sub is None else sub), h], dev)

        def got(ox, oy, half, sub):
            h = ox * 4 + oy
            view = unit(h, half, sub)
            arrived(view, sends.at[0], recv.at[half * 2 + (0 if sub is None else sub), h])

        def coords(half, first, second):
            return (xs[first], ys[second]) if half == 0 else (xs[second], ys[first])

        def devs(half):
            return ((x_up, x_dn), (y_up, y_dn)) if half == 0 else ((y_up, y_dn), (x_up, x_dn))

        def own():
            for half in (0, 1):
                for dev in devs(half)[0]:
                    push(x, y, half, None, dev)
            for half in (0, 1):
                for dev in devs(half)[1]:
                    push(x, y, half, None, dev)

        def first_near():
            for half in (0, 1):
                (up1, dn1), (up2, dn2) = devs(half)
                ox, oy = coords(half, 3, 0)
                got(ox, oy, half, None)
                push(ox, oy, half, 0, up1)
                push(ox, oy, half, None, up2)
                push(ox, oy, half, None, dn2)
                ox, oy = coords(half, 1, 0)
                got(ox, oy, half, None)
                push(ox, oy, half, 1, dn1)
                push(ox, oy, half, None, up2)
                push(ox, oy, half, None, dn2)

        def second(first):
            def run():
                for half in (0, 1):
                    (up1, dn1), (up2, dn2) = devs(half)
                    ox, oy = coords(half, first, 3)
                    got(ox, oy, half, None)
                    if first in (0, 1):
                        push(ox, oy, half, None, up2)
                    ox, oy = coords(half, first, 1)
                    got(ox, oy, half, None)
                    if first in (2, 3):
                        push(ox, oy, half, None, dn2)
            return run

        def first_far():
            for half in (0, 1):
                (up1, dn1), (up2, dn2) = devs(half)
                ox, oy = coords(half, 2, 0)
                for sub in (0, 1):
                    got(ox, oy, half, sub)
                push(ox, oy, half, None, up2)
                push(ox, oy, half, None, dn2)

        def last():
            for half in (0, 1):
                for first in range(4):
                    ox, oy = coords(half, first, 2)
                    got(ox, oy, half, None)

        return [own, first_near, second(0), second(3), second(1), first_far, second(2), last]

    def x_unit(h, half, sub):
        if sub is None:
            return x_all.at[h, pl.ds(64 * half, 64)]
        return x_all.at[h, pl.ds(64 * half + 32 * sub, 32)]

    def c_unit(h, half, sub):
        cols = pl.ds(pl.multiple_of((h // 8) * 256, 256), 256)
        if sub is None:
            return ct.at[pl.ds(4 * half, 4), c, h % 8, :, cols]
        return ct.at[pl.ds(4 * half + 2 * sub, 2), c, h % 8, :, cols]

    def ring(buf, recv, sends, first_src):
        count = [0]

        def push(src, dst, dev):
            i = count[0]
            count[0] += 1
            send(src, buf.at[dst], sends.at[i], recv.at[dst], dev)

        def got(s):
            arrived(buf.at[s], sends.at[0], recv.at[s])

        def own():
            push(first_src, seq, partner)
            push(buf.at[seq], seq, z_up)
            push(buf.at[seq], seq, z_dn)

        def mate():
            s = z * 2 + other
            got(s)
            push(buf.at[s], s, z_up)
            push(buf.at[s], s, z_dn)

        def hop(d, p):
            def run():
                parity = c if p == 0 else other
                if d < 4:
                    below, above = zs[8 - d] * 2 + parity, zs[d] * 2 + parity
                    got(below)
                    if d < 3 or p == 0:
                        push(buf.at[below], below, z_up)
                    got(above)
                    if d < 3 or p == 1:
                        push(buf.at[above], above, z_dn)
                else:
                    got(zs[4] * 2 + parity)
            return run

        return [own, mate] + [hop(d, p) for d in (1, 2, 3, 4) for p in (0, 1)]

    a_steps = plane(x_unit, x_recv, x_send)
    c_steps = plane(c_unit, c_recv, c_send)
    l_steps = ring(lsb, l_recv, l_send, lsb.at[seq])
    u_steps = ring(upb, u_recv, u_send, up_x)
    g_steps = ring(qkv, g_recv, g_send, qkv_x)

    a_steps[0]()
    l_steps[0]()
    u_steps[0]()
    l_steps[1]()
    u_steps[1]()
    a_steps[1]()
    for i in range(4):
        l_steps[2 + 2 * i]()
        l_steps[3 + 2 * i]()
        u_steps[2 + 2 * i]()
        u_steps[3 + 2 * i]()
        a_steps[2 + i]()
    a_steps[6]()
    a_steps[7]()

    half_h, group = head // 8, head % 8
    cols = pl.ds(pl.multiple_of(half_h * 256, 256), 256)

    def slice_of(zt):
        return x_all.at[2 * zt + half_h, pl.ds(pl.multiple_of(group * 16, 16), 16)]

    own_slice = pltpu.make_async_copy(slice_of(z), ct.at[z, c, group, :, cols], loc.at[6])
    own_slice.start()
    for i in range(1, 8):
        send(slice_of(zs[i]), ct.at[z, c, group, :, cols], z_send.at[i], z_recv.at[z], at(dz=zs[i]))

    for i in range(3):
        weights[i].wait()
    for i in range(3):
        acc = dot(x_all[0], w_all[i, 0:256, :], 1, 0)
        for h in range(1, 16):
            acc = acc + dot(x_all[h], w_all[i, 256 * h : 256 * (h + 1), :], 1, 0)
        acc = acc.astype(BF16)
        qkv[seq, i] = jnp.where(c == 0, acc[:, :128], acc[:, 128:])
        qkv_x[i] = jnp.where(c == 0, acc[:, 128:], acc[:, :128])
    g_steps[0]()

    ti = lax.broadcasted_iota(jnp.int32, (128, 128), 0)
    si = lax.broadcasted_iota(jnp.int32, (128, 128), 1)

    def attend(b):
        q, k, v, u = qkv[b, 0], qkv[b, 1], qkv[b, 2], upb[b]
        sums = lsb[b]
        row = jnp.where(c == 0, sums[0:1], sums[1:2])
        before = segs[jnp.maximum(b * 128 - 1, 0)]
        previous = jnp.where(b > 0, before, -1).astype(F32)
        last = segs[b * 128 + 127].astype(F32)
        ls_s = jnp.broadcast_to(row, (128, 128))
        ls_t = ls_s.T
        seg_s = jnp.broadcast_to(segv[pl.ds(b, 1), :], (128, 128)).astype(F32)
        seg_t = seg_s.T
        same = (seg_s == seg_t) & (ti >= si)
        decay = jnp.where(same, SCALE * jnp.exp(jnp.where(same, ls_t - ls_s, 0.0)), 0.0)
        ls_last = row[:, 127:128]
        inflow = jnp.where(seg_t == previous, jnp.exp(ls_t), 0.0)
        outflow = jnp.where(seg_t == last, jnp.exp(ls_last - ls_t), 0.0)
        keep = jnp.where(last == previous, jnp.exp(ls_last), 0.0)
        carry[b] = jnp.broadcast_to(keep, (8, 128))
        inm[b] = inflow
        outm[b] = outflow
        a_qk = (decay * dot(q, k, 1, 1)).astype(BF16)
        a_up = (decay * dot(u, v, 1, 1)).astype(BF16)
        gl[b, 0] = dot(a_up, k, 1, 0)
        gl[b, 1] = dot(a_up, q, 0, 0)
        gl[b, 2] = dot(a_qk, u, 0, 0)
        wk_ = (SCALE * outflow * k.astype(F32)).astype(BF16)
        wq_ = (SCALE * inflow * q.astype(F32)).astype(BF16)
        lst[b] = dot(wk_, v, 0, 0)
        rst[b] = dot(wq_, u, 0, 0)

    def c_local():
        own_slice.wait()
        for i in range(1, 8):
            arrived(ct.at[zs[i], c, group, :, cols], z_send.at[0], z_recv.at[zs[i]])

    def c_share():
        for i in range(4):
            view = ct.at[pl.ds(2 * i, 2), c]
            send(view, view, d_send.at[i], d_recv.at[i], partner)

    side = [c_local] + c_steps + [c_share]

    g_steps[1]()
    side.pop(0)()
    side.pop(0)()

    def pair(b0, b1):
        def body(i, carry_):
            attend(jnp.where(i == 0, b0, b1))
            return carry_
        lax.fori_loop(0, 2, body, 0)

    pair(seq, z * 2 + other)
    for d in (1, 2, 3):
        for p in (0, 1):
            g_steps[2 + 2 * (d - 1) + p]()
            parity = c if p == 0 else other
            pair(zs[8 - d] * 2 + parity, zs[d] * 2 + parity)
            if side:
                side.pop(0)()
            if side and d == 2:
                side.pop(0)()
    while side:
        side.pop(0)()
    g_steps[8]()
    g_steps[9]()
    pair(zs[4] * 2, zs[4] * 2 + 1)
    for i in range(4):
        arrived(ct.at[pl.ds(2 * i, 2), other], d_send.at[0], d_recv.at[i])

    def forward(b, state):
        inc[b] = state.astype(BF16)
        return carry[b][0:1] * state + lst[b]

    lax.fori_loop(0, 16, forward, jnp.zeros((128, 128), F32))

    def backward(i, state):
        b = 15 - i
        ret[b] = state.astype(BF16)
        return carry[b][0:1] * state + rst[b]

    lax.fori_loop(0, 16, backward, jnp.zeros((128, 128), F32))

    def finish(b, carry_):
        inflow, outflow = inm[b], outm[b]
        grad[b, :, 0:128] = (gl[b, 0] + inflow * dot(upb[b], inc[b], 1, 1)).astype(BF16)
        grad[b, :, 128:256] = (gl[b, 1] + outflow * dot(qkv[b, 2], ret[b], 1, 1)).astype(BF16)
        grad[b, :, 256:384] = (gl[b, 2] + outflow * dot(qkv[b, 1], ret[b], 1, 0)).astype(BF16)
        return carry_

    lax.fori_loop(0, 16, finish, 0)

    def rows_of(core):
        left = ct[:, :, :, :, pl.ds(pl.multiple_of(core * 256, 256), 256)].reshape(2048, 256)
        return dot(left, grad[...].reshape(2048, 384), 0, 0).astype(BF16)

    rows_x[...] = rows_of(other)
    send(rows_x, rows_r, o_send.at[0], o_recv.at[0], partner)
    mine = rows_of(c)
    arrived(rows_r, o_send.at[0], o_recv.at[0])
    theirs = rows_r[...]
    for i, out in enumerate((out_q, out_k, out_v)):
        a, b = mine[:, 128 * i : 128 * (i + 1)], theirs[:, 128 * i : 128 * (i + 1)]
        out[:, 0:128] = jnp.where(c == 0, a, b)
        out[:, 128:256] = jnp.where(c == 0, b, a)
    for copy in sent:
        copy.wait_send()


def local(tokens, w_query, w_key, w_value, upstream, log_decay, segment):
    anyspace = pl.BlockSpec(memory_space=pl.ANY)
    vmem = pl.BlockSpec(memory_space=pltpu.VMEM)
    smem = pl.BlockSpec(memory_space=pltpu.SMEM)
    dma = pltpu.SemaphoreType.DMA
    out = jax.ShapeDtypeStruct((256, 256), BF16)
    return pl.pallas_call(
        kernel,
        out_shape=(out, out, out),
        in_specs=[anyspace] * 5 + [vmem, vmem, smem],
        out_specs=(vmem, vmem, vmem),
        scratch_shapes=[
            pltpu.VMEM((16, 128, 256), BF16),
            pltpu.VMEM((3, 4096, 256), BF16),
            pltpu.VMEM((16, 3, 128, 128), BF16),
            pltpu.VMEM((3, 128, 128), BF16),
            pltpu.VMEM((16, 128, 128), BF16),
            pltpu.VMEM((128, 128), BF16),
            pltpu.VMEM((16, 8, 128), F32),
            pltpu.VMEM((8, 2, 8, 16, 512), BF16),
            pltpu.VMEM((16, 3, 128, 128), F32),
            pltpu.VMEM((16, 128, 128), F32),
            pltpu.VMEM((16, 128, 128), F32),
            pltpu.VMEM((16, 8, 128), F32),
            pltpu.VMEM((16, 128, 128), F32),
            pltpu.VMEM((16, 128, 128), F32),
            pltpu.VMEM((16, 128, 128), BF16),
            pltpu.VMEM((16, 128, 128), BF16),
            pltpu.VMEM((16, 128, 384), BF16),
            pltpu.VMEM((256, 384), BF16),
            pltpu.VMEM((256, 384), BF16),
            dma((4, 16)), dma((32,)),
            dma((4, 16)), dma((32,)),
            dma((8,)), dma((8,)),
            dma((16,)), dma((15,)),
            dma((16,)), dma((15,)),
            dma((16,)), dma((15,)),
            dma((4,)), dma((4,)),
            dma((1,)), dma((1,)),
            dma((7,)),
        ],
        compiler_params=pltpu.CompilerParams(
            collective_id=0, has_side_effects=True, vmem_limit_bytes=60 * 1024 * 1024
        ),
    )(
        tokens, w_query, w_key, w_value, upstream,
        log_decay.T, segment.reshape(16, 128), segment,
    )


def solution(mesh):
    in_specs = (
        P("seq", "head"), P(None, "head"), P(None, "head"), P(None, "head"),
        P("seq", "head"), P("seq", "head"), P(),
    )
    out_specs = (P("seq", "head"),) * 3
    return jax.shard_map(local, mesh=mesh, in_specs=in_specs, out_specs=out_specs, check_vma=False)
```

time: 222 us -> 71.9 us (0.32)
  blocking collectives: 115 us -> 0 us
  Pallas kernels: 0 us -> 66.4 us
  local copies, waits for them, and re-layouts: 42.9 us -> 4.7 us
  waiting for transfers between devices: 17.1 us -> 0 us
  between operations: 15.7 us -> 0.64 us
  matrix products: 13 us -> 0 us
  other arithmetic: 9.77 us -> 0 us
  starting transfers between devices: 7.61 us -> 0 us
    all_gather x6 -> x0, blocking collectives: 70.2 us -> none  [prefix_by_axis(): lax.all_gather(part.astype(kind), axis)]
    pallas_call x0 -> x1, Pallas kernels: none -> 66.4 us  [local(): pl.pallas_call(kernel, out_shape=(out, out, out), in_specs=[anyspace] * 5...]
    all_to_all x1 -> x0, blocking collectives: 44.5 us -> none  [local(): lax.all_to_all(piece, SEQ, split_axis=1, concat_axis=0, tiled=True)]
    unnamed x51 -> x3, local copies, waits for them, and re-layouts: 32.5 us -> 4.7 us
    all_gather x1 -> x0, waiting for transfers between devices: 17.1 us -> none  [local(): every = lax.all_gather(grads, SEQ, axis=0, tiled=True)]
    dot_general x13 -> x0, matrix products: 13 us -> none  [the longest x1 2.87 us: local(): lax.dot_general(columns, every, contract, preferred_element_type=jnp.floa...]
    all_to_all x1 -> x0, starting transfers between devices: 7.57 us -> none  [copy_for_each(): lax.all_to_all(jnp.broadcast_to(x[None], (count, *x.shape)), axis, 0, 0,...]
    convert_element_type x5 -> x0, other arithmetic: 4.19 us -> none  [the longest x3 2.98 us: prefix_by_axis(): part.astype(kind)]
  transfers between devices with their start and end apart: 2 -> 0, of which waited for: 1 -> 0; matrix products, arithmetic and copies ran while one was open for 4% -> 0% of each run, Pallas kernels for 0% -> 0%
where the time goes in v1:
time: 71.9 us; the launch traced here: 71.7 us
  Pallas kernels  66.4 us (92%)
  local copies, waits for them, and re-layouts  4.7 us (7%)
    pallas_call x1, Pallas kernels, local(): pl.pallas_call(kernel, out_shape=(out, out, out), in_specs=[anyspace] * 5...  66.4 us
    unnamed x3, local copies, waits for them, and re-layouts  4.7 us

profile of v1, /device:TPU:1, one launch (start us, length us, event | category | flops | bytes accessed | tf_op | source)
XLA Modules:
  0.0 71.7 jit_solution(14877030101511488407)
XLA Ops:
  0.6 66.4 %shard_map.94 = (bf16[256,256]{1,0:T(8,128)(2,1)}, bf16[256,256]{1,0:T(8,128)(2,1)}, bf16[256,256]{1,0:T(8,128)(2,1)}) custom-call(bf16[128,256]{1,0:T(8,128)(2,1)} %tok.1, bf16[4096,256]{1,0:T(8,128)(2,1)} %wq.1, bf16[4096,256]{1,0:T(8,128)(2,1)} %wk.1, bf16[4096,256]{1,0:T(8,128)(2,1)} %wv.1, bf16[128,256]{1,0:T(8,128)(2,1)} %up.1, f32[2,128]{1,0:T(2,128)} %bitcast.3, ...), custom_call_target="tpu_custom_call" | custom-call | tf_op jit(solution)/shard_map/pallas_call | solution.py:374
  67.0 1.6 %copy.13 = bf16[256,256]{1,0:T(8,128)(2,1)} copy(bf16[256,256]{1,0:T(8,128)(2,1)} %get-tuple-element.6) | data formatting | bytes 262144
  68.6 1.6 %copy.14 = bf16[256,256]{1,0:T(8,128)(2,1)} copy(bf16[256,256]{1,0:T(8,128)(2,1)} %get-tuple-element.7) | data formatting | bytes 262144
  70.1 1.6 %copy.15 = bf16[256,256]{1,0:T(8,128)(2,1)} copy(bf16[256,256]{1,0:T(8,128)(2,1)} %get-tuple-element.8) | data formatting | bytes 262144

commit v2 on v1

v2 whole, which is shorter than its diff:
```python
import functools

import jax
import jax.numpy as jnp
from jax import lax
from jax.experimental import pallas as pl
from jax.experimental.pallas import tpu as pltpu
from jax.sharding import PartitionSpec as P

HEAD = 128
SCALE = HEAD ** (-0.5)
MESH = pl.DeviceIdType.MESH
BF16, F32 = jnp.bfloat16, jnp.float32


def dot(a, b, da, db):
    return lax.dot_general(a, b, (((da,), (db,)), ((), ())), preferred_element_type=F32)


def kernel(
    tok, wq, wk, wv, up, ldt_in, segv_in, segs_in,
    out,
    ldt, segv, segs, x_all, w_all, qkv, qkv_x, upb, up_x, ct,
    gl, inm, outm, carry, lst, rst, inc, ret, grad, rows_x, rows_r,
    x_recv, x_send, c_recv, c_send, z_recv, z_send, u_recv, u_send,
    g_recv, g_send, d_recv, d_send, o_recv, o_send, loc,
):
    seq, head = lax.axis_index("seq"), lax.axis_index("head")
    z, c = seq // 2, seq % 2
    x, y = head // 4, head % 4
    other = 1 - c

    def at(dz=None, core=None, hx=None, hy=None):
        zz = z if dz is None else dz
        cc = c if core is None else core
        xx = x if hx is None else hx
        yy = y if hy is None else hy
        return {"seq": zz * 2 + cc, "head": xx * 4 + yy}

    xs = [(x + i) % 4 for i in range(4)]
    ys = [(y + i) % 4 for i in range(4)]
    zs = [(z + i) % 8 for i in range(8)]
    partner = at(core=other)
    x_up, x_dn, y_up, y_dn = at(hx=xs[1]), at(hx=xs[3]), at(hy=ys[1]), at(hy=ys[3])
    z_up, z_dn = at(dz=zs[1]), at(dz=zs[7])

    sent = []

    def send(src, dst, ssem, rsem, dev):
        copy = pltpu.make_async_remote_copy(
            src_ref=src, dst_ref=dst, send_sem=ssem, recv_sem=rsem, device_id=dev, device_id_type=MESH
        )
        copy.start()
        sent.append(copy)

    def arrived(dst, ssem, rsem):
        pltpu.make_async_remote_copy(
            src_ref=dst, dst_ref=dst, send_sem=ssem, recv_sem=rsem, device_id=partner, device_id_type=MESH
        ).wait_recv()

    barrier = pltpu.get_barrier_semaphore()
    near = [partner, x_up, x_dn, y_up, y_dn] + [at(dz=zs[i]) for i in range(1, 8)]
    for dev in near:
        pl.semaphore_signal(barrier, inc=1, device_id=dev, device_id_type=MESH)

    def fetch(src, dst, i):
        copy = pltpu.make_async_copy(src, dst, loc.at[i])
        copy.start()
        return copy

    def lanes(i):
        return pl.ds(pl.multiple_of(i * 128, 128), 128)

    own_tok = fetch(tok, x_all.at[head], 0)
    own_ldt = fetch(ldt_in, ldt, 1)
    own_up = fetch(up.at[:, lanes(c)], upb.at[seq, 0:128], 2)
    oth_up = fetch(up.at[:, lanes(other)], up_x.at[0:128], 3)
    seg_v = fetch(segv_in, segv, 4)
    seg_s = fetch(segs_in, segs, 5)
    weights = [fetch(w, w_all.at[i], 7 + i) for i, w in enumerate((wq, wk, wv))]

    own_ldt.wait()
    total = jnp.concatenate([ldt[...], jnp.zeros((6, 128), F32)], axis=0)
    lane = lax.broadcasted_iota(jnp.int32, (8, 128), 1)
    for k in (1, 2, 4, 8, 16, 32, 64):
        total = total + jnp.where(lane >= k, pltpu.roll(total, k, 1), 0.0)

    def in_parts(row):
        hi = row.astype(BF16)
        rest = row - hi.astype(F32)
        mid = rest.astype(BF16)
        low = (rest - mid.astype(F32)).astype(BF16)
        return jnp.concatenate([hi.astype(F32), mid.astype(F32), low.astype(F32), jnp.zeros((13, 128), F32)], axis=0).astype(BF16)

    lo, hi = in_parts(total[0:1]), in_parts(total[1:2])
    upb[seq, 128:144] = jnp.where(c == 0, lo, hi)
    up_x[128:144] = jnp.where(c == 0, hi, lo)

    own_tok.wait()
    pl.semaphore_wait(barrier, len(near))

    def plane(unit, recv, sends):
        count = [0]

        def push(ox, oy, half, sub, dev):
            h = ox * 4 + oy
            i = count[0]
            count[0] += 1
            view = unit(h, half, sub)
            send(view, view, sends.at[i], recv.at[half * 2 + (0 if sub is None else sub), h], dev)

        def got(ox, oy, half, sub):
            h = ox * 4 + oy
            view = unit(h, half, sub)
            arrived(view, sends.at[0], recv.at[half * 2 + (0 if sub is None else sub), h])

        def coords(half, first, second):
            return (xs[first], ys[second]) if half == 0 else (xs[second], ys[first])

        def devs(half):
            return ((x_up, x_dn), (y_up, y_dn)) if half == 0 else ((y_up, y_dn), (x_up, x_dn))

        def own():
            for half in (0, 1):
                for dev in devs(half)[0]:
                    push(x, y, half, None, dev)
            for half in (0, 1):
                for dev in devs(half)[1]:
                    push(x, y, half, None, dev)

        def first_near():
            for half in (0, 1):
                (up1, dn1), (up2, dn2) = devs(half)
                ox, oy = coords(half, 3, 0)
                got(ox, oy, half, None)
                push(ox, oy, half, 0, up1)
                push(ox, oy, half, None, up2)
                push(ox, oy, half, None, dn2)
                ox, oy = coords(half, 1, 0)
                got(ox, oy, half, None)
                push(ox, oy, half, 1, dn1)
                push(ox, oy, half, None, up2)
                push(ox, oy, half, None, dn2)

        def second(first):
            def run():
                for half in (0, 1):
                    (up1, dn1), (up2, dn2) = devs(half)
                    ox, oy = coords(half, first, 3)
                    got(ox, oy, half, None)
                    if first in (0, 1):
                        push(ox, oy, half, None, up2)
                    ox, oy = coords(half, first, 1)
                    got(ox, oy, half, None)
                    if first in (2, 3):
                        push(ox, oy, half, None, dn2)
            return run

        def first_far():
            for half in (0, 1):
                (up1, dn1), (up2, dn2) = devs(half)
                ox, oy = coords(half, 2, 0)
                for sub in (0, 1):
                    got(ox, oy, half, sub)
                push(ox, oy, half, None, up2)
                push(ox, oy, half, None, dn2)

        def last(first):
            def run():
                for half in (0, 1):
                    ox, oy = coords(half, first, 2)
                    got(ox, oy, half, None)
            return run

        return [
            [own],
            [first_near, second(0)],
            [first_far, second(3), second(1), last(0)],
            [second(2), last(1), last(3)],
            [last(2)],
        ]

    def x_unit(h, half, sub):
        if sub is None:
            return x_all.at[h, pl.ds(64 * half, 64)]
        return x_all.at[h, pl.ds(64 * half + 32 * sub, 32)]

    def c_unit(h, half, sub):
        if sub is None:
            return ct.at[h // 8, pl.ds(4 * half, 4), c, h % 8]
        return ct.at[h // 8, pl.ds(4 * half + 2 * sub, 2), c, h % 8]

    def ring(buf, recv, sends, first_src):
        count = [0]

        def push(src, dst, dev):
            i = count[0]
            count[0] += 1
            send(src, buf.at[dst], sends.at[i], recv.at[dst], dev)

        def got(s):
            arrived(buf.at[s], sends.at[0], recv.at[s])

        def own():
            push(first_src, seq, partner)
            push(buf.at[seq], seq, z_up)
            push(buf.at[seq], seq, z_dn)

        def mate():
            s = z * 2 + other
            got(s)
            push(buf.at[s], s, z_up)
            push(buf.at[s], s, z_dn)

        def hop(d, p):
            def run():
                parity = c if p == 0 else other
                if d < 4:
                    below, above = zs[8 - d] * 2 + parity, zs[d] * 2 + parity
                    got(below)
                    if d < 3 or p == 0:
                        push(buf.at[below], below, z_up)
                    got(above)
                    if d < 3 or p == 1:
                        push(buf.at[above], above, z_dn)
                else:
                    got(zs[4] * 2 + parity)
            return run

        return [own, mate] + [hop(d, p) for d in (1, 2, 3, 4) for p in (0, 1)]

    a_steps = plane(x_unit, x_recv, x_send)
    c_steps = plane(c_unit, c_recv, c_send)
    u_steps = ring(upb, u_recv, u_send, up_x)
    g_steps = ring(qkv, g_recv, g_send, qkv_x)

    def run(steps):
        for step in steps:
            step()

    run(a_steps[0])
    own_up.wait()
    oth_up.wait()
    run(u_steps[0:2])
    run(a_steps[1])
    run(u_steps[2:4])
    run(a_steps[2])
    run(u_steps[4:6])
    run(a_steps[3])
    run(a_steps[4])

    half_h, group = head // 8, head % 8

    def slice_of(zt):
        return x_all.at[2 * zt + half_h, pl.ds(pl.multiple_of(group * 16, 16), 16)]

    own_slice = pltpu.make_async_copy(slice_of(z), ct.at[half_h, z, c, group], loc.at[6])
    own_slice.start()
    for i in range(1, 8):
        send(slice_of(zs[i]), ct.at[half_h, z, c, group], z_send.at[i], z_recv.at[z], at(dz=zs[i]))

    for copy in weights:
        copy.wait()
    seg_v.wait()
    seg_s.wait()
    for i in range(3):
        acc = dot(x_all[0], w_all[i, 0:256, :], 1, 0)
        for h in range(1, 16):
            acc = acc + dot(x_all[h], w_all[i, 256 * h : 256 * (h + 1), :], 1, 0)
        acc = acc.astype(BF16)
        qkv[seq, i] = jnp.where(c == 0, acc[:, :128], acc[:, 128:])
        qkv_x[i] = jnp.where(c == 0, acc[:, 128:], acc[:, :128])
    g_steps[0]()
    run(u_steps[6:8])
    g_steps[1]()

    ti = lax.broadcasted_iota(jnp.int32, (128, 128), 0)
    si = lax.broadcasted_iota(jnp.int32, (128, 128), 1)

    def attend(blocks):
        done = []
        for b in blocks:
            q, k, v, u = qkv[b, 0], qkv[b, 1], qkv[b, 2], upb[b, 0:128]
            parts = upb[b, 128:144].astype(F32)
            row = parts[0:1] + parts[1:2] + parts[2:3]
            before = segs[jnp.maximum(b * 128 - 1, 0)]
            previous = jnp.where(b > 0, before, -1).astype(F32)
            last = segs[b * 128 + 127].astype(F32)
            ls_s = jnp.broadcast_to(row, (128, 128))
            ls_t = ls_s.T
            seg_s = jnp.broadcast_to(segv[pl.ds(b, 1), :], (128, 128)).astype(F32)
            seg_t = seg_s.T
            same = (seg_s == seg_t) & (ti >= si)
            decay = jnp.where(same, SCALE * jnp.exp(jnp.where(same, ls_t - ls_s, 0.0)), 0.0)
            ls_last = row[:, 127:128]
            inflow = jnp.where(seg_t == previous, jnp.exp(ls_t), 0.0)
            outflow = jnp.where(seg_t == last, jnp.exp(ls_last - ls_t), 0.0)
            keep = jnp.where(last == previous, jnp.exp(ls_last), 0.0)
            a_qk = (decay * dot(q, k, 1, 1)).astype(BF16)
            a_up = (decay * dot(u, v, 1, 1)).astype(BF16)
            wk_ = (SCALE * outflow * k.astype(F32)).astype(BF16)
            wq_ = (SCALE * inflow * q.astype(F32)).astype(BF16)
            done.append((
                inflow, outflow, jnp.broadcast_to(keep, (8, 128)), dot(a_up, k, 1, 0), dot(a_up, q, 0, 0),
                dot(a_qk, u, 0, 0), dot(wk_, v, 0, 0), dot(wq_, u, 0, 0),
            ))
        for b, (inflow, outflow, keep, gq, gk, gv, ls, rs) in zip(blocks, done):
            inm[b], outm[b], carry[b] = inflow, outflow, keep
            gl[b, 0], gl[b, 1], gl[b, 2] = gq, gk, gv
            lst[b], rst[b] = ls, rs

    def c_local():
        own_slice.wait()
        for i in range(1, 8):
            arrived(ct.at[half_h, zs[i], c, group], z_send.at[0], z_recv.at[zs[i]])

    def c_share():
        for i in range(4):
            view = ct.at[:, pl.ds(2 * i, 2), c]
            send(view, view, d_send.at[i], d_recv.at[i], partner)

    side = [[c_local] + c_steps[0]] + c_steps[1:] + [[c_share]]

    attend((seq, z * 2 + other))
    run(side[0])
    n = 1
    for d in (1, 2, 3):
        for p in (0, 1):
            g_steps[2 + 2 * (d - 1) + p]()
            parity = c if p == 0 else other
            attend((zs[8 - d] * 2 + parity, zs[d] * 2 + parity))
            if n < len(side):
                run(side[n])
                n += 1
            if d == 1 and p == 1:
                run(u_steps[8:10])
    for i in range(4):
        arrived(ct.at[:, pl.ds(2 * i, 2), other], d_send.at[0], d_recv.at[i])
    g_steps[8]()
    g_steps[9]()
    attend((zs[4] * 2, zs[4] * 2 + 1))

    def forward(b, state):
        inc[b] = state.astype(BF16)
        return carry[b][0:1] * state + lst[b]

    lax.fori_loop(0, 16, forward, jnp.zeros((128, 128), F32))

    def backward(i, state):
        b = 15 - i
        ret[b] = state.astype(BF16)
        return carry[b][0:1] * state + rst[b]

    lax.fori_loop(0, 16, backward, jnp.zeros((128, 128), F32))

    def finish(i, carry_):
        done = []
        for b in (4 * i, 4 * i + 1, 4 * i + 2, 4 * i + 3):
            inflow, outflow = inm[b], outm[b]
            done.append((
                gl[b, 0] + inflow * dot(upb[b, 0:128], inc[b], 1, 1),
                gl[b, 1] + outflow * dot(qkv[b, 2], ret[b], 1, 1),
                gl[b, 2] + outflow * dot(qkv[b, 1], ret[b], 1, 0),
            ))
        for j, parts in enumerate(done):
            for k, part in enumerate(parts):
                grad[4 * i + j, :, 128 * k : 128 * (k + 1)] = part.astype(BF16)
        return carry_

    lax.fori_loop(0, 4, finish, 0)

    def rows_of(core):
        return dot(ct[core].reshape(2048, 256), grad[...].reshape(2048, 384), 0, 0).astype(BF16)

    rows_x[...] = rows_of(other)
    send(rows_x, rows_r, o_send.at[0], o_recv.at[0], partner)
    mine = rows_of(c)
    for i in range(3):
        out[i, :, lanes(c)] = mine[:, 128 * i : 128 * (i + 1)]
    arrived(rows_r, o_send.at[0], o_recv.at[0])
    for i in range(3):
        out[i, :, lanes(other)] = rows_r[:, 128 * i : 128 * (i + 1)]
    for copy in sent:
        copy.wait_send()


def local(tokens, w_query, w_key, w_value, upstream, log_decay, segment):
    hbm = pl.BlockSpec(memory_space=pltpu.HBM)
    dma = pltpu.SemaphoreType.DMA
    out = pl.pallas_call(
        kernel,
        out_shape=jax.ShapeDtypeStruct((3, 256, 256), BF16),
        in_specs=[hbm] * 8,
        out_specs=pl.BlockSpec(memory_space=pltpu.VMEM),
        scratch_shapes=[
            pltpu.VMEM((2, 128), F32),
            pltpu.VMEM((16, 128), jnp.int32),
            pltpu.SMEM((2048,), jnp.int32),
            pltpu.VMEM((16, 128, 256), BF16),
            pltpu.VMEM((3, 4096, 256), BF16),
            pltpu.VMEM((16, 3, 128, 128), BF16),
            pltpu.VMEM((3, 128, 128), BF16),
            pltpu.VMEM((16, 144, 128), BF16),
            pltpu.VMEM((144, 128), BF16),
            pltpu.VMEM((2, 8, 2, 8, 16, 256), BF16),
            pltpu.VMEM((16, 3, 128, 128), F32),
            pltpu.VMEM((16, 128, 128), F32),
            pltpu.VMEM((16, 128, 128), F32),
            pltpu.VMEM((16, 8, 128), F32),
            pltpu.VMEM((16, 128, 128), F32),
            pltpu.VMEM((16, 128, 128), F32),
            pltpu.VMEM((16, 128, 128), BF16),
            pltpu.VMEM((16, 128, 128), BF16),
            pltpu.VMEM((16, 128, 384), BF16),
            pltpu.VMEM((256, 384), BF16),
            pltpu.VMEM((256, 384), BF16),
            dma((4, 16)), dma((32,)),
            dma((4, 16)), dma((32,)),
            dma((8,)), dma((8,)),
            dma((16,)), dma((15,)),
            dma((16,)), dma((15,)),
            dma((4,)), dma((4,)),
            dma((1,)), dma((1,)),
            dma((10,)),
        ],
        compiler_params=pltpu.CompilerParams(
            collective_id=0, has_side_effects=True, vmem_limit_bytes=60 * 1024 * 1024
        ),
    )(
        tokens, w_query, w_key, w_value, upstream,
        log_decay.T, segment.reshape(16, 128), segment,
    )
    return out[0], out[1], out[2]


def solution(mesh):
    in_specs = (
        P("seq", "head"), P(None, "head"), P(None, "head"), P(None, "head"),
        P("seq", "head"), P("seq", "head"), P(),
    )
    out_specs = (P("seq", "head"),) * 3
    return jax.shard_map(local, mesh=mesh, in_specs=in_specs, out_specs=out_specs, check_vma=False)
```

time: 71.9 us -> 58.3 us (0.81)
  Pallas kernels: 66.4 us -> 55.7 us
  local copies, waits for them, and re-layouts: 4.7 us -> 1.78 us
    pallas_call x1, Pallas kernels: 66.4 us -> 55.7 us  [local(): pl.pallas_call(kernel, out_shape=jax.ShapeDtypeStruct((3, 256, 256), BF16...]
    unnamed x3 -> x0, local copies, waits for them, and re-layouts: 4.7 us -> none
    squeeze x0 -> x1, local copies, waits for them, and re-layouts: none -> 1.78 us  [local(): return (out[0], out[1], out[2])]
where the time goes in v2:
time: 58.3 us; the launch traced here: 58.2 us
  Pallas kernels  55.7 us (96%)
  local copies, waits for them, and re-layouts  1.78 us (3%)
  between operations  0.64 us (1%)
    pallas_call x1, Pallas kernels, local(): pl.pallas_call(kernel, out_shape=jax.ShapeDtypeStruct((3, 256, 256), BF16...  55.7 us
    squeeze x1, local copies, waits for them, and re-layouts, local(): return (out[0], out[1], out[2])  1.78 us

profile of v2, /device:TPU:1, one launch (start us, length us, event | category | flops | bytes accessed | tf_op | source)
XLA Modules:
  0.0 58.2 jit_solution(15656506833783600469)
XLA Ops:
  0.6 55.7 %shard_map.94 = bf16[3,256,256]{2,1,0:T(8,128)(2,1)} custom-call(bf16[128,256]{1,0:T(8,128)(2,1)} %tok.1, bf16[4096,256]{1,0:T(8,128)(2,1)} %wq.1, bf16[4096,256]{1,0:T(8,128)(2,1)} %wk.1, bf16[4096,256]{1,0:T(8,128)(2,1)} %wv.1, bf16[128,256]{1,0:T(8,128)(2,1)} %up.1, f32[2,128]{1,0:T(2,128)} %bitcast.9, s32[16,128]{1,0:T(8,128)} %bitcast.8, s32[2048]{0:T(1024)} %segs_in.1), custom_call_target="tpu_custom_call" | custom-call | tf_op jit(solution)/shard_map/pallas_call | solution.py:390
  56.4 1.8 %slice_bitcast_fusion = (bf16[256,256]{1,0:T(8,128)(2,1)}, bf16[256,256]{1,0:T(8,128)(2,1)}, bf16[256,256]{1,0:T(8,128)(2,1)}) fusion(bf16[3,256,256]{2,1,0:T(8,128)(2,1)} %shard_map.94), kind=kLoop, calls=%fused_computation | loop fusion | bytes 786432 | tf_op jit(solution)/shard_map/squeeze | solution.py:433

commit v3 on v2

v3 whole, which is shorter than its diff:
```python
import jax
import jax.numpy as jnp
from jax import lax
from jax.experimental import pallas as pl
from jax.experimental.pallas import tpu as pltpu
from jax.sharding import PartitionSpec as P

HEAD = 128
SCALE = HEAD ** (-0.5)
MESH = pl.DeviceIdType.MESH
BF16, F32 = jnp.bfloat16, jnp.float32
AROUND = (1, 3, 2)


def dot(a, b, da, db):
    return lax.dot_general(a, b, (((da,), (db,)), ((), ())), preferred_element_type=F32)


def kernel(
    tok, wq, wk, wv, up, ldt_in, segv_in, segs_in,
    out,
    ldt, segv, segs, x_all, w_all, qkv, qkv_x, upb, up_x, ct,
    gl, inm, outm, carry, lst, rst, inc, ret, grad, rows_x, rows_r,
    x_first, x_rest, c_first, c_rest, z_recv, u_recv, g_mate, g_recv, d_recv, o_recv, sends, loc,
):
    seq, head = lax.axis_index("seq"), lax.axis_index("head")
    z, c = seq // 2, seq % 2
    x, y = head // 4, head % 4
    other = 1 - c
    zs = [(z + i) % 8 for i in range(8)]

    def plane_at(dx, dy):
        return ((x + dx) % 4) * 4 + (y + dy) % 4

    def at(dz=0, dx=0, dy=0, core=None):
        return {"seq": zs[dz] * 2 + (c if core is None else core), "head": plane_at(dx, dy)}

    partner = at(core=other)
    barrier = pltpu.get_barrier_semaphore()
    near = [partner] + [at(dx=i) for i in AROUND] + [at(dy=i) for i in AROUND] + [at(dz=i) for i in range(1, 8)]
    for dev in near:
        pl.semaphore_signal(barrier, inc=1, device_id=dev, device_id_type=MESH)

    def fetch(src, dst, i):
        copy = pltpu.make_async_copy(src, dst, loc.at[i])
        copy.start()
        return copy

    def lanes(i):
        return pl.ds(pl.multiple_of(i * 128, 128), 128)

    own_tok = [fetch(tok.at[:, 128 * i : 128 * (i + 1)], x_all.at[i, head], i) for i in range(2)]
    own_ldt = fetch(ldt_in, ldt, 2)
    own_up = fetch(up.at[:, lanes(c)], upb.at[seq, 0:128], 3)
    oth_up = fetch(up.at[:, lanes(other)], up_x.at[0:128], 4)
    seg_v = fetch(segv_in, segv, 5)
    seg_s = fetch(segs_in, segs, 6)
    weights = [fetch(w, w_all.at[i], 7 + i) for i, w in enumerate((wq, wk, wv))]

    own_ldt.wait()
    total = jnp.concatenate([ldt[...], jnp.zeros((6, 128), F32)], axis=0)
    lane = lax.broadcasted_iota(jnp.int32, (8, 128), 1)
    for k in (1, 2, 4, 8, 16, 32, 64):
        total = total + jnp.where(lane >= k, pltpu.roll(total, k, 1), 0.0)

    def in_parts(row):
        hi = row.astype(BF16)
        rest = row - hi.astype(F32)
        mid = rest.astype(BF16)
        low = (rest - mid.astype(F32)).astype(BF16)
        return jnp.concatenate([hi.astype(F32), mid.astype(F32), low.astype(F32), jnp.zeros((13, 128), F32)], axis=0).astype(BF16)

    lo, hi = in_parts(total[0:1]), in_parts(total[1:2])
    upb[seq, 128:144] = jnp.where(c == 0, lo, hi)
    up_x[128:144] = jnp.where(c == 0, hi, lo)

    for copy in own_tok:
        copy.wait()
    pl.semaphore_wait(barrier, len(near))

    sent = {}

    def send(kind, src, dst, recv, dev):
        rows = src.dtype.itemsize
        for n in src.shape:
            rows *= n
        sent[kind] = sent.get(kind, 0) + rows // 512
        pltpu.make_async_remote_copy(
            src_ref=src, dst_ref=dst, send_sem=sends.at[kind], recv_sem=recv, device_id=dev, device_id_type=MESH
        ).start()

    def described(view, recv):
        return pltpu.make_async_remote_copy(
            src_ref=view, dst_ref=view, send_sem=sends.at[0], recv_sem=recv, device_id=partner, device_id_type=MESH
        )

    def arrived(view, recv):
        described(view, recv).wait_recv()

    def arrived_rows(rows, recv):
        arrived(w_all.at[0, 0:rows], recv)

    def plane(kind, unit, rows, first, rest):
        def there(half, stage, d):
            return at(dx=d) if half == stage else at(dy=d)

        def own():
            for half in (0, 1):
                for j, d in enumerate(AROUND):
                    view = unit(head, half)
                    send(kind, view, view, first.at[half, j], there(half, 0, d))
            for half in (0, 1):
                for d in AROUND:
                    view = unit(head, half)
                    send(kind, view, view, rest, there(half, 1, d))

        def middle():
            for j, d in enumerate(AROUND):
                for half in (0, 1):
                    view = unit(plane_at(-d, 0) if half == 0 else plane_at(0, -d), half)
                    arrived(view, first.at[half, j])
                    for e in AROUND:
                        send(kind, view, view, rest, there(half, 1, e))

        def end():
            arrived_rows(24 * rows, rest)

        return own, middle, end

    def x_unit(k):
        return lambda h, half: x_all.at[half, h, 64 * k : 64 * (k + 1)]

    def c_unit(h, half):
        return ct.at[h // 8, (h // 4) % 2, 4 * half : 4 * (half + 1), c, h % 4]

    def up_own():
        send(2, up_x, upb.at[seq], u_recv.at[8], partner)
        send(2, upb.at[seq], upb.at[seq], u_recv.at[0], at(dz=1))
        send(2, upb.at[seq], upb.at[seq], u_recv.at[4], at(dz=7))

    def up_mate():
        s = z * 2 + other
        arrived(upb.at[s], u_recv.at[8])
        send(2, upb.at[s], upb.at[s], u_recv.at[0], at(dz=1))
        send(2, upb.at[s], upb.at[s], u_recv.at[4], at(dz=7))

    def up_hop(d):
        below, above = zs[8 - d] * 2, zs[d] * 2
        count = 2 if d < 4 else 1
        arrived(upb.at[0:count], u_recv.at[d - 1])
        if d < 4:
            for parity in (c, other) if d < 3 else (c,):
                send(2, upb.at[below + parity], upb.at[below + parity], u_recv.at[d], at(dz=1))
        arrived(upb.at[0:count], u_recv.at[4 + d - 1])
        if d < 4:
            for parity in (c, other) if d < 3 else (other,):
                send(2, upb.at[above + parity], upb.at[above + parity], u_recv.at[4 + d], at(dz=7))

    def g_to_next(s, p, k, d, both=True, down=False):
        view = qkv.at[s, k]
        if both or not down:
            send(3, view, view, g_recv.at[((0 * 4 + d) * 2 + p) * 2 + k], at(dz=1))
        if both or down:
            send(3, view, view, g_recv.at[((1 * 4 + d) * 2 + p) * 2 + k], at(dz=7))

    def g_own(k):
        send(3, qkv_x.at[k], qkv.at[seq, k], g_mate.at[k], partner)
        g_to_next(seq, 0, k, 0)

    def g_from_mate(k):
        s = z * 2 + other
        arrived(qkv.at[s, k], g_mate.at[k])
        g_to_next(s, 1, k, 0)

    def g_hop(d, p, k):
        parity = c if p == 0 else other
        if d < 4 or p == 0:
            s = zs[8 - d] * 2 + parity
            arrived(qkv.at[s, k], g_recv.at[((0 * 4 + d - 1) * 2 + p) * 2 + k])
            if d < 3 or (d == 3 and p == 0):
                g_to_next(s, p, k, d, both=False)
        if d < 4 or p == 1:
            s = zs[d] * 2 + parity
            arrived(qkv.at[s, k], g_recv.at[((1 * 4 + d - 1) * 2 + p) * 2 + k])
            if d < 3 or (d == 3 and p == 1):
                g_to_next(s, p, k, d, both=False, down=True)

    def project(k):
        for i in range(3):
            acc = jnp.zeros((64, 256), F32)
            for h in range(16):
                left = jnp.concatenate([x_all[j, h, 64 * k : 64 * (k + 1)] for j in (0, 1)], axis=1)
                acc = acc + dot(left, w_all[i, 256 * h : 256 * (h + 1), :], 1, 0)
            acc = acc.astype(BF16)
            qkv[seq, k, i] = jnp.where(c == 0, acc[:, :128], acc[:, 128:])
            qkv_x[k, i] = jnp.where(c == 0, acc[:, 128:], acc[:, :128])

    a_own, a_mid, a_end = zip(*[plane(0, x_unit(k), 32, x_first.at[k], x_rest.at[k]) for k in (0, 1)])
    c_own, c_mid, c_end = plane(1, c_unit, 64, c_first, c_rest)

    a_own[0]()
    a_own[1]()
    own_up.wait()
    oth_up.wait()
    up_own()
    up_mate()
    a_mid[0]()
    a_mid[1]()
    up_hop(1)
    for copy in weights:
        copy.wait()
    seg_v.wait()
    seg_s.wait()
    a_end[0]()
    project(0)
    g_own(0)
    g_from_mate(0)
    up_hop(2)
    a_end[1]()

    f, hb, rg = head // 8, (head // 4) % 2, head % 4

    def slice_of(zt):
        return x_all.at[hb, 2 * zt + f, pl.ds(pl.multiple_of(rg * 32, 32), 32)]

    own_slice = fetch(slice_of(z), ct.at[f, hb, z, c, rg], 0)
    for i in range(1, 8):
        send(4, slice_of(zs[i]), ct.at[f, hb, z, c, rg], z_recv.at[0], at(dz=i))
    project(1)
    g_own(1)
    g_from_mate(1)
    up_hop(3)

    ti = lax.broadcasted_iota(jnp.int32, (128, 128), 0)
    si = lax.broadcasted_iota(jnp.int32, (128, 128), 1)

    def part(b, i):
        return jnp.concatenate([qkv[b, 0, i], qkv[b, 1, i]], axis=0)

    def attend(blocks):
        done = []
        for b in blocks:
            q, k, v, u = part(b, 0), part(b, 1), part(b, 2), upb[b, 0:128]
            parts = upb[b, 128:144].astype(F32)
            row = parts[0:1] + parts[1:2] + parts[2:3]
            before = segs[jnp.maximum(b * 128 - 1, 0)]
            previous = jnp.where(b > 0, before, -1).astype(F32)
            last = segs[b * 128 + 127].astype(F32)
            ls_s = jnp.broadcast_to(row, (128, 128))
            ls_t = ls_s.T
            seg_s = jnp.broadcast_to(segv[pl.ds(b, 1), :], (128, 128)).astype(F32)
            seg_t = seg_s.T
            same = (seg_s == seg_t) & (ti >= si)
            decay = jnp.where(same, SCALE * jnp.exp(jnp.where(same, ls_t - ls_s, 0.0)), 0.0)
            ls_last = row[:, 127:128]
            inflow = jnp.where(seg_t == previous, jnp.exp(ls_t), 0.0)
            outflow = jnp.where(seg_t == last, jnp.exp(ls_last - ls_t), 0.0)
            keep = jnp.where(last == previous, jnp.exp(ls_last), 0.0)
            a_qk = (decay * dot(q, k, 1, 1)).astype(BF16)
            a_up = (decay * dot(u, v, 1, 1)).astype(BF16)
            wk_ = (SCALE * outflow * k.astype(F32)).astype(BF16)
            wq_ = (SCALE * inflow * q.astype(F32)).astype(BF16)
            done.append((
                inflow, outflow, jnp.broadcast_to(keep, (8, 128)), dot(a_up, k, 1, 0), dot(a_up, q, 0, 0),
                dot(a_qk, u, 0, 0), dot(wk_, v, 0, 0), dot(wq_, u, 0, 0),
            ))
        for b, (inflow, outflow, keep, gq, gk, gv, ls, rs) in zip(blocks, done):
            inm[b], outm[b], carry[b] = inflow, outflow, keep
            gl[b, 0], gl[b, 1], gl[b, 2] = gq, gk, gv
            lst[b], rst[b] = ls, rs

    def c_begin():
        own_slice.wait()
        arrived_rows(7 * 16, z_recv.at[0])
        c_own()

    def c_share():
        c_end()
        for i in (0, 1):
            view = ct.at[i, :, :, c]
            send(5, view, view, d_recv.at[i], partner)

    def up_last():
        up_hop(4)

    attend((seq, z * 2 + other))
    side = {(1, 0): c_begin, (1, 1): up_last, (2, 0): c_mid, (3, 1): c_share}
    for d in (1, 2, 3):
        for p in (0, 1):
            parity = c if p == 0 else other
            if p == 0:
                g_hop(d, 0, 0)
                g_hop(d, 1, 0)
            g_hop(d, p, 1)
            attend((zs[8 - d] * 2 + parity, zs[d] * 2 + parity))
            if (d, p) in side:
                side[d, p]()
    for p in (0, 1):
        for k in (0, 1):
            g_hop(4, p, k)
    attend((zs[4] * 2, zs[4] * 2 + 1))

    def forward(b, state):
        inc[b] = state.astype(BF16)
        return carry[b][0:1] * state + lst[b]

    lax.fori_loop(0, 16, forward, jnp.zeros((128, 128), F32))

    def backward(i, state):
        b = 15 - i
        ret[b] = state.astype(BF16)
        return carry[b][0:1] * state + rst[b]

    lax.fori_loop(0, 16, backward, jnp.zeros((128, 128), F32))

    def finish(i, carry_):
        done = []
        for b in (4 * i, 4 * i + 1, 4 * i + 2, 4 * i + 3):
            inflow, outflow = inm[b], outm[b]
            done.append((
                gl[b, 0] + inflow * dot(upb[b, 0:128], inc[b], 1, 1),
                gl[b, 1] + outflow * dot(part(b, 2), ret[b], 1, 1),
                gl[b, 2] + outflow * dot(part(b, 1), ret[b], 1, 0),
            ))
        for j, parts in enumerate(done):
            for k, value in enumerate(parts):
                grad[4 * i + j, :, 128 * k : 128 * (k + 1)] = value.astype(BF16)
        return carry_

    lax.fori_loop(0, 4, finish, 0)
    for i in (0, 1):
        arrived(ct.at[i, :, :, other], d_recv.at[i])

    def rows_of(core):
        left = jnp.concatenate([ct[core, j].reshape(2048, 128) for j in (0, 1)], axis=1)
        return dot(left, grad[...].reshape(2048, 384), 0, 0).astype(BF16)

    rows_x[...] = rows_of(other)
    send(6, rows_x, rows_r, o_recv.at[0], partner)
    mine = rows_of(c)
    for i in range(3):
        out[i, :, lanes(c)] = mine[:, 128 * i : 128 * (i + 1)]
    arrived(rows_r, o_recv.at[0])
    for i in range(3):
        out[i, :, lanes(other)] = rows_r[:, 128 * i : 128 * (i + 1)]
    for kind, rows in sent.items():
        view = w_all.at[0, 0:rows]
        pltpu.make_async_remote_copy(
            src_ref=view, dst_ref=view, send_sem=sends.at[kind], recv_sem=loc.at[0], device_id=partner, device_id_type=MESH
        ).wait_send()


def local(tokens, w_query, w_key, w_value, upstream, log_decay, segment):
    hbm = pl.BlockSpec(memory_space=pltpu.HBM)
    dma = pltpu.SemaphoreType.DMA
    out = pl.pallas_call(
        kernel,
        out_shape=jax.ShapeDtypeStruct((3, 256, 256), BF16),
        in_specs=[hbm] * 8,
        out_specs=pl.BlockSpec(memory_space=pltpu.VMEM),
        scratch_shapes=[
            pltpu.VMEM((2, 128), F32),
            pltpu.VMEM((16, 128), jnp.int32),
            pltpu.SMEM((2048,), jnp.int32),
            pltpu.VMEM((2, 16, 128, 128), BF16),
            pltpu.VMEM((3, 4096, 256), BF16),
            pltpu.VMEM((16, 2, 3, 64, 128), BF16),
            pltpu.VMEM((2, 3, 64, 128), BF16),
            pltpu.VMEM((16, 144, 128), BF16),
            pltpu.VMEM((144, 128), BF16),
            pltpu.VMEM((2, 2, 8, 2, 4, 32, 128), BF16),
            pltpu.VMEM((16, 3, 128, 128), F32),
            pltpu.VMEM((16, 128, 128), F32),
            pltpu.VMEM((16, 128, 128), F32),
            pltpu.VMEM((16, 8, 128), F32),
            pltpu.VMEM((16, 128, 128), F32),
            pltpu.VMEM((16, 128, 128), F32),
            pltpu.VMEM((16, 128, 128), BF16),
            pltpu.VMEM((16, 128, 128), BF16),
            pltpu.VMEM((16, 128, 384), BF16),
            pltpu.VMEM((256, 384), BF16),
            pltpu.VMEM((256, 384), BF16),
            dma((2, 2, 3)), dma((2,)),
            dma((2, 3)), dma(()),
            dma((1,)), dma((9,)),
            dma((2,)), dma((32,)),
            dma((2,)), dma((1,)),
            dma((7,)), dma((10,)),
        ],
        compiler_params=pltpu.CompilerParams(
            collective_id=0, has_side_effects=True, vmem_limit_bytes=60 * 1024 * 1024
        ),
    )(
        tokens, w_query, w_key, w_value, upstream,
        log_decay.T, segment.reshape(16, 128), segment,
    )
    return out[0], out[1], out[2]


def solution(mesh):
    in_specs = (
        P("seq", "head"), P(None, "head"), P(None, "head"), P(None, "head"),
        P("seq", "head"), P("seq", "head"), P(),
    )
    out_specs = (P("seq", "head"),) * 3
    return jax.shard_map(local, mesh=mesh, in_specs=in_specs, out_specs=out_specs, check_vma=False)
```

time: 58.3 us -> 50.6 us (0.87)
  Pallas kernels: 55.7 us -> 48.1 us
    pallas_call x1, Pallas kernels: 55.7 us -> 48.1 us  [local(): pl.pallas_call(kernel, out_shape=jax.ShapeDtypeStruct((3, 256, 256), BF16...]
where the time goes in v3:
time: 50.6 us; the launch traced here: 50.5 us
  Pallas kernels  48.1 us (95%)
  local copies, waits for them, and re-layouts  1.78 us (4%)
  between operations  0.64 us (1%)
    pallas_call x1, Pallas kernels, local(): pl.pallas_call(kernel, out_shape=jax.ShapeDtypeStruct((3, 256, 256), BF16...  48.1 us
    squeeze x1, local copies, waits for them, and re-layouts, local(): return (out[0], out[1], out[2])  1.78 us

profile of v3, /device:TPU:1, one launch (start us, length us, event | category | flops | bytes accessed | tf_op | source)
XLA Modules:
  0.0 50.5 jit_solution(17955691388986774218)
XLA Ops:
  0.6 48.1 %shard_map.94 = bf16[3,256,256]{2,1,0:T(8,128)(2,1)} custom-call(bf16[128,256]{1,0:T(8,128)(2,1)} %tok.1, bf16[4096,256]{1,0:T(8,128)(2,1)} %wq.1, bf16[4096,256]{1,0:T(8,128)(2,1)} %wk.1, bf16[4096,256]{1,0:T(8,128)(2,1)} %wv.1, bf16[128,256]{1,0:T(8,128)(2,1)} %up.1, f32[2,128]{1,0:T(2,128)} %bitcast.9, s32[16,128]{1,0:T(8,128)} %bitcast.8, s32[2048]{0:T(1024)} %segs_in.1), custom_call_target="tpu_custom_call" | custom-call | tf_op jit(solution)/shard_map/pallas_call | solution.py:356
  48.7 1.8 %slice_bitcast_fusion = (bf16[256,256]{1,0:T(8,128)(2,1)}, bf16[256,256]{1,0:T(8,128)(2,1)}, bf16[256,256]{1,0:T(8,128)(2,1)}) fusion(bf16[3,256,256]{2,1,0:T(8,128)(2,1)} %shard_map.94), kind=kLoop, calls=%fused_computation | loop fusion | bytes 786432 | tf_op jit(solution)/shard_map/squeeze | solution.py:397

commit v4 on v3

--- a/solution.py
+++ b/solution.py
@@ -21,7 +21,7 @@
     out,
     ldt, segv, segs, x_all, w_all, qkv, qkv_x, upb, up_x, ct,
     gl, inm, outm, carry, lst, rst, inc, ret, grad, rows_x, rows_r,
-    x_first, x_rest, c_first, c_rest, z_recv, u_recv, g_mate, g_recv, d_recv, o_recv, sends, loc,
+    x_first, x_rest, c_first, c_rest, z_recv, u_recv, g_mate, g_recv, d_recv, o_recv, sends, loc, alive,
 ):
     seq, head = lax.axis_index("seq"), lax.axis_index("head")
     z, c = seq // 2, seq % 2
@@ -37,7 +37,7 @@
 
     partner = at(core=other)
     barrier = pltpu.get_barrier_semaphore()
-    near = [partner] + [at(dx=i) for i in AROUND] + [at(dy=i) for i in AROUND] + [at(dz=i) for i in range(1, 8)]
+    near = [partner] + [at(dx=i) for i in AROUND] + [at(dy=i) for i in AROUND] + [at(dz=i, core=j) for i in (1, 7) for j in (c, other)]
     for dev in near:
         pl.semaphore_signal(barrier, inc=1, device_id=dev, device_id_type=MESH)
 
@@ -49,7 +49,7 @@
     def lanes(i):
         return pl.ds(pl.multiple_of(i * 128, 128), 128)
 
-    own_tok = [fetch(tok.at[:, 128 * i : 128 * (i + 1)], x_all.at[i, head], i) for i in range(2)]
+    own_tok = fetch(tok, x_all.at[head], 0)
     own_ldt = fetch(ldt_in, ldt, 2)
     own_up = fetch(up.at[:, lanes(c)], upb.at[seq, 0:128], 3)
     oth_up = fetch(up.at[:, lanes(other)], up_x.at[0:128], 4)
@@ -57,25 +57,7 @@
     seg_s = fetch(segs_in, segs, 6)
     weights = [fetch(w, w_all.at[i], 7 + i) for i, w in enumerate((wq, wk, wv))]
 
-    own_ldt.wait()
-    total = jnp.concatenate([ldt[...], jnp.zeros((6, 128), F32)], axis=0)
-    lane = lax.broadcasted_iota(jnp.int32, (8, 128), 1)
-    for k in (1, 2, 4, 8, 16, 32, 64):
-        total = total + jnp.where(lane >= k, pltpu.roll(total, k, 1), 0.0)
-
-    def in_parts(row):
-        hi = row.astype(BF16)
-        rest = row - hi.astype(F32)
-        mid = rest.astype(BF16)
-        low = (rest - mid.astype(F32)).astype(BF16)
-        return jnp.concatenate([hi.astype(F32), mid.astype(F32), low.astype(F32), jnp.zeros((13, 128), F32)], axis=0).astype(BF16)
-
-    lo, hi = in_parts(total[0:1]), in_parts(total[1:2])
-    upb[seq, 128:144] = jnp.where(c == 0, lo, hi)
-    up_x[128:144] = jnp.where(c == 0, hi, lo)
-
-    for copy in own_tok:
-        copy.wait()
+    own_tok.wait()
     pl.semaphore_wait(barrier, len(near))
 
     sent = {}
@@ -128,21 +110,16 @@
         return own, middle, end
 
     def x_unit(k):
-        return lambda h, half: x_all.at[half, h, 64 * k : 64 * (k + 1)]
+        return lambda h, half: x_all.at[h, 64 * half + 32 * k : 64 * half + 32 * (k + 1)]
 
     def c_unit(h, half):
-        return ct.at[h // 8, (h // 4) % 2, 4 * half : 4 * (half + 1), c, h % 4]
+        return ct.at[h // 8, 4 * half : 4 * (half + 1), c, h % 8]
 
     def up_own():
         send(2, up_x, upb.at[seq], u_recv.at[8], partner)
-        send(2, upb.at[seq], upb.at[seq], u_recv.at[0], at(dz=1))
-        send(2, upb.at[seq], upb.at[seq], u_recv.at[4], at(dz=7))
-
-    def up_mate():
-        s = z * 2 + other
-        arrived(upb.at[s], u_recv.at[8])
-        send(2, upb.at[s], upb.at[s], u_recv.at[0], at(dz=1))
-        send(2, upb.at[s], upb.at[s], u_recv.at[4], at(dz=7))
+        for i, j in ((1, 0), (7, 4)):
+            send(2, upb.at[seq], upb.at[seq], u_recv.at[j], at(dz=i))
+            send(2, up_x, upb.at[seq], u_recv.at[j], at(dz=i, core=other))
 
     def up_hop(d):
         below, above = zs[8 - d] * 2, zs[d] * 2
@@ -156,92 +133,112 @@
             for parity in (c, other) if d < 3 else (other,):
                 send(2, upb.at[above + parity], upb.at[above + parity], u_recv.at[4 + d], at(dz=7))
 
-    def g_to_next(s, p, k, d, both=True, down=False):
-        view = qkv.at[s, k]
+    def g_to_next(s, p, i, d, both=True, down=False):
+        view = qkv.at[s, i]
         if both or not down:
-            send(3, view, view, g_recv.at[((0 * 4 + d) * 2 + p) * 2 + k], at(dz=1))
+            send(3, view, view, g_recv.at[((0 * 4 + d) * 2 + p) * 3 + i], at(dz=1))
         if both or down:
-            send(3, view, view, g_recv.at[((1 * 4 + d) * 2 + p) * 2 + k], at(dz=7))
-
-    def g_own(k):
-        send(3, qkv_x.at[k], qkv.at[seq, k], g_mate.at[k], partner)
-        g_to_next(seq, 0, k, 0)
-
-    def g_from_mate(k):
-        s = z * 2 + other
-        arrived(qkv.at[s, k], g_mate.at[k])
-        g_to_next(s, 1, k, 0)
-
-    def g_hop(d, p, k):
+            send(3, view, view, g_recv.at[((1 * 4 + d) * 2 + p) * 3 + i], at(dz=7))
+
+    def g_own():
+        for i in range(3):
+            g_to_next(seq, 0, i, 0)
+        for i in range(3):
+            send(3, qkv_x.at[i], qkv.at[seq, i], g_mate.at[i], partner)
+            for j, dz in ((0, 1), (1, 7)):
+                send(3, qkv_x.at[i], qkv.at[seq, i], g_recv.at[(j * 4 * 2 + 1) * 3 + i], at(dz=dz, core=other))
+
+    def g_from_mate():
+        for i in range(3):
+            arrived(qkv.at[z * 2 + other, i], g_mate.at[i])
+        arrived(upb.at[z * 2 + other], u_recv.at[8])
+
+    def g_hop(d, p):
         parity = c if p == 0 else other
-        if d < 4 or p == 0:
-            s = zs[8 - d] * 2 + parity
-            arrived(qkv.at[s, k], g_recv.at[((0 * 4 + d - 1) * 2 + p) * 2 + k])
-            if d < 3 or (d == 3 and p == 0):
-                g_to_next(s, p, k, d, both=False)
-        if d < 4 or p == 1:
-            s = zs[d] * 2 + parity
-            arrived(qkv.at[s, k], g_recv.at[((1 * 4 + d - 1) * 2 + p) * 2 + k])
-            if d < 3 or (d == 3 and p == 1):
-                g_to_next(s, p, k, d, both=False, down=True)
-
-    def project(k):
         for i in range(3):
-            acc = jnp.zeros((64, 256), F32)
-            for h in range(16):
-                left = jnp.concatenate([x_all[j, h, 64 * k : 64 * (k + 1)] for j in (0, 1)], axis=1)
-                acc = acc + dot(left, w_all[i, 256 * h : 256 * (h + 1), :], 1, 0)
+            if d < 4 or p == 0:
+                s = zs[8 - d] * 2 + parity
+                arrived(qkv.at[s, i], g_recv.at[((0 * 4 + d - 1) * 2 + p) * 3 + i])
+                if d < 3 or (d == 3 and p == 0):
+                    g_to_next(s, p, i, d, both=False)
+            if d < 4 or p == 1:
+                s = zs[d] * 2 + parity
+                arrived(qkv.at[s, i], g_recv.at[((1 * 4 + d - 1) * 2 + p) * 3 + i])
+                if d < 3 or (d == 3 and p == 1):
+                    g_to_next(s, p, i, d, both=False, down=True)
+
+    def project():
+        for i in range(3):
+            acc = dot(x_all[0], w_all[i, 0:256, :], 1, 0)
+            for h in range(1, 16):
+                acc = acc + dot(x_all[h], w_all[i, 256 * h : 256 * (h + 1), :], 1, 0)
             acc = acc.astype(BF16)
-            qkv[seq, k, i] = jnp.where(c == 0, acc[:, :128], acc[:, 128:])
-            qkv_x[k, i] = jnp.where(c == 0, acc[:, 128:], acc[:, :128])
+            qkv[seq, i] = jnp.where(c == 0, acc[:, :128], acc[:, 128:])
+            qkv_x[i] = jnp.where(c == 0, acc[:, 128:], acc[:, :128])
 
     a_own, a_mid, a_end = zip(*[plane(0, x_unit(k), 32, x_first.at[k], x_rest.at[k]) for k in (0, 1)])
     c_own, c_mid, c_end = plane(1, c_unit, 64, c_first, c_rest)
 
     a_own[0]()
     a_own[1]()
+
+    own_ldt.wait()
+    total = jnp.concatenate([ldt[...], jnp.zeros((6, 128), F32)], axis=0)
+    lane = lax.broadcasted_iota(jnp.int32, (8, 128), 1)
+    for k in (1, 2, 4, 8, 16, 32, 64):
+        total = total + jnp.where(lane >= k, pltpu.roll(total, k, 1), 0.0)
+
+    def in_parts(row):
+        hi = row.astype(BF16)
+        rest = row - hi.astype(F32)
+        mid = rest.astype(BF16)
+        low = (rest - mid.astype(F32)).astype(BF16)
+        return jnp.concatenate([hi.astype(F32), mid.astype(F32), low.astype(F32), jnp.zeros((5, 128), F32)], axis=0).astype(BF16)
+
+    lo, hi = in_parts(total[0:1]), in_parts(total[1:2])
+    upb[seq, 128:136] = jnp.where(c == 0, lo, hi)
+    up_x[128:136] = jnp.where(c == 0, hi, lo)
+
     own_up.wait()
     oth_up.wait()
     up_own()
-    up_mate()
     a_mid[0]()
     a_mid[1]()
     up_hop(1)
+    for i in (2, 6):
+        pl.semaphore_signal(alive, inc=1, device_id=at(dz=i), device_id_type=MESH)
     for copy in weights:
         copy.wait()
     seg_v.wait()
     seg_s.wait()
     a_end[0]()
-    project(0)
-    g_own(0)
-    g_from_mate(0)
     up_hop(2)
     a_end[1]()
 
-    f, hb, rg = head // 8, (head // 4) % 2, head % 4
+    f, group = head // 8, head % 8
 
     def slice_of(zt):
-        return x_all.at[hb, 2 * zt + f, pl.ds(pl.multiple_of(rg * 32, 32), 32)]
-
-    own_slice = fetch(slice_of(z), ct.at[f, hb, z, c, rg], 0)
-    for i in range(1, 8):
-        send(4, slice_of(zs[i]), ct.at[f, hb, z, c, rg], z_recv.at[0], at(dz=i))
-    project(1)
-    g_own(1)
-    g_from_mate(1)
-    up_hop(3)
+        return x_all.at[2 * zt + f, pl.ds(pl.multiple_of(group * 16, 16), 16)]
+
+    own_slice = fetch(slice_of(z), ct.at[f, z, c, group], 0)
+    pl.semaphore_wait(alive, 2)
+    for i in (4, 3, 5, 2, 6, 1, 7):
+        send(4, slice_of(zs[i]), ct.at[f, z, c, group], z_recv.at[0], at(dz=i))
+    project()
+    g_own()
+    g_from_mate()
 
     ti = lax.broadcasted_iota(jnp.int32, (128, 128), 0)
     si = lax.broadcasted_iota(jnp.int32, (128, 128), 1)
 
     def part(b, i):
-        return jnp.concatenate([qkv[b, 0, i], qkv[b, 1, i]], axis=0)
+        return qkv[b, i]
 
     def attend(blocks):
         done = []
         for b in blocks:
             q, k, v, u = part(b, 0), part(b, 1), part(b, 2), upb[b, 0:128]
-            parts = upb[b, 128:144].astype(F32)
+            parts = upb[b, 128:136].astype(F32)
             row = parts[0:1] + parts[1:2] + parts[2:3]
             before = segs[jnp.maximum(b * 128 - 1, 0)]
             previous = jnp.where(b > 0, before, -1).astype(F32)
@@ -277,27 +274,24 @@
     def c_share():
         c_end()
         for i in (0, 1):
-            view = ct.at[i, :, :, c]
+            view = ct.at[i, :, c]
             send(5, view, view, d_recv.at[i], partner)
 
-    def up_last():
-        up_hop(4)
-
     attend((seq, z * 2 + other))
-    side = {(1, 0): c_begin, (1, 1): up_last, (2, 0): c_mid, (3, 1): c_share}
+    side = {(1, 0): c_begin, (2, 0): c_mid, (3, 1): c_share}
     for d in (1, 2, 3):
         for p in (0, 1):
             parity = c if p == 0 else other
-            if p == 0:
-                g_hop(d, 0, 0)
-                g_hop(d, 1, 0)
-            g_hop(d, p, 1)
+            g_hop(d, p)
             attend((zs[8 - d] * 2 + parity, zs[d] * 2 + parity))
+            if (d, p) == (1, 1):
+                up_hop(3)
+            if (d, p) == (3, 0):
+                up_hop(4)
             if (d, p) in side:
                 side[d, p]()
     for p in (0, 1):
-        for k in (0, 1):
-            g_hop(4, p, k)
+        g_hop(4, p)
     attend((zs[4] * 2, zs[4] * 2 + 1))
 
     def forward(b, state):
@@ -329,11 +323,10 @@
 
     lax.fori_loop(0, 4, finish, 0)
     for i in (0, 1):
-        arrived(ct.at[i, :, :, other], d_recv.at[i])
+        arrived(ct.at[i, :, other], d_recv.at[i])
 
     def rows_of(core):
-        left = jnp.concatenate([ct[core, j].reshape(2048, 128) for j in (0, 1)], axis=1)
-        return dot(left, grad[...].reshape(2048, 384), 0, 0).astype(BF16)
+        return dot(ct[core].reshape(2048, 256), grad[...].reshape(2048, 384), 0, 0).astype(BF16)
 
     rows_x[...] = rows_of(other)
     send(6, rows_x, rows_r, o_recv.at[0], partner)
@@ -344,7 +337,7 @@
     for i in range(3):
         out[i, :, lanes(other)] = rows_r[:, 128 * i : 128 * (i + 1)]
     for kind, rows in sent.items():
-        view = w_all.at[0, 0:rows]
+        view = upb.at[0:15] if kind == 2 else w_all.at[0, 0:rows]
         pltpu.make_async_remote_copy(
             src_ref=view, dst_ref=view, send_sem=sends.at[kind], recv_sem=loc.at[0], device_id=partner, device_id_type=MESH
         ).wait_send()
@@ -362,13 +355,13 @@
             pltpu.VMEM((2, 128), F32),
             pltpu.VMEM((16, 128), jnp.int32),
             pltpu.SMEM((2048,), jnp.int32),
-            pltpu.VMEM((2, 16, 128, 128), BF16),
+            pltpu.VMEM((16, 128, 256), BF16),
             pltpu.VMEM((3, 4096, 256), BF16),
-            pltpu.VMEM((16, 2, 3, 64, 128), BF16),
-            pltpu.VMEM((2, 3, 64, 128), BF16),
-            pltpu.VMEM((16, 144, 128), BF16),
-            pltpu.VMEM((144, 128), BF16),
-            pltpu.VMEM((2, 2, 8, 2, 4, 32, 128), BF16),
+            pltpu.VMEM((16, 3, 128, 128), BF16),
+            pltpu.VMEM((3, 128, 128), BF16),
+            pltpu.VMEM((16, 136, 128), BF16),
+            pltpu.VMEM((136, 128), BF16),
+            pltpu.VMEM((2, 8, 2, 8, 16, 256), BF16),
             pltpu.VMEM((16, 3, 128, 128), F32),
             pltpu.VMEM((16, 128, 128), F32),
             pltpu.VMEM((16, 128, 128), F32),
@@ -383,9 +376,10 @@
             dma((2, 2, 3)), dma((2,)),
             dma((2, 3)), dma(()),
             dma((1,)), dma((9,)),
-            dma((2,)), dma((32,)),
+            dma((3,)), dma((48,)),
             dma((2,)), dma((1,)),
             dma((7,)), dma((10,)),
+            pltpu.SemaphoreType.REGULAR,
         ],
         compiler_params=pltpu.CompilerParams(
             collective_id=0, has_side_effects=True, vmem_limit_bytes=60 * 1024 * 1024

time: 50.6 us -> 48 us (0.949)
  Pallas kernels: 48.1 us -> 45.5 us
    pallas_call x1, Pallas kernels: 48.1 us -> 45.5 us  [local(): pl.pallas_call(kernel, out_shape=jax.ShapeDtypeStruct((3, 256, 256), BF16...]
where the time goes in v4:
time: 48 us; the launch traced here: 47.9 us
  Pallas kernels  45.5 us (95%)
  local copies, waits for them, and re-layouts  1.78 us (4%)
  between operations  0.64 us (1%)
    pallas_call x1, Pallas kernels, local(): pl.pallas_call(kernel, out_shape=jax.ShapeDtypeStruct((3, 256, 256), BF16...  45.5 us
    squeeze x1, local copies, waits for them, and re-layouts, local(): return (out[0], out[1], out[2])  1.78 us

profile of v4, /device:TPU:1, one launch (start us, length us, event | category | flops | bytes accessed | tf_op | source)
XLA Modules:
  0.0 47.9 jit_solution(10668295270601266671)
XLA Ops:
  0.6 45.5 %shard_map.94 = bf16[3,256,256]{2,1,0:T(8,128)(2,1)} custom-call(bf16[128,256]{1,0:T(8,128)(2,1)} %tok.1, bf16[4096,256]{1,0:T(8,128)(2,1)} %wq.1, bf16[4096,256]{1,0:T(8,128)(2,1)} %wk.1, bf16[4096,256]{1,0:T(8,128)(2,1)} %wv.1, bf16[128,256]{1,0:T(8,128)(2,1)} %up.1, f32[2,128]{1,0:T(2,128)} %bitcast.9, s32[16,128]{1,0:T(8,128)} %bitcast.8, s32[2048]{0:T(1024)} %segs_in.1), custom_call_target="tpu_custom_call" | custom-call | tf_op jit(solution)/shard_map/pallas_call | solution.py:349
  46.1 1.8 %slice_bitcast_fusion = (bf16[256,256]{1,0:T(8,128)(2,1)}, bf16[256,256]{1,0:T(8,128)(2,1)}, bf16[256,256]{1,0:T(8,128)(2,1)}) fusion(bf16[3,256,256]{2,1,0:T(8,128)(2,1)} %shard_map.94), kind=kLoop, calls=%fused_computation | loop fusion | bytes 786432 | tf_op jit(solution)/shard_map/squeeze | solution.py:391

commit v5 on v4

--- a/solution.py
+++ b/solution.py
@@ -20,7 +20,7 @@
     tok, wq, wk, wv, up, ldt_in, segv_in, segs_in,
     out,
     ldt, segv, segs, x_all, w_all, qkv, qkv_x, upb, up_x, ct,
-    gl, inm, outm, carry, lst, rst, inc, ret, grad, rows_x, rows_r,
+    gl, inm, outm, carry, dec, lst, rst, inc, ret, grad, rows_x, rows_r,
     x_first, x_rest, c_first, c_rest, z_recv, u_recv, g_mate, g_recv, d_recv, o_recv, sends, loc, alive,
 ):
     seq, head = lax.axis_index("seq"), lax.axis_index("head")
@@ -142,30 +142,35 @@
 
     def g_own():
         for i in range(3):
-            g_to_next(seq, 0, i, 0)
+            g_to_next(seq, 0, i, 0, both=False)
+            send(3, qkv_x.at[i], qkv.at[seq, i], g_recv.at[(1 * 4 * 2 + 1) * 3 + i], at(dz=7, core=other))
         for i in range(3):
             send(3, qkv_x.at[i], qkv.at[seq, i], g_mate.at[i], partner)
-            for j, dz in ((0, 1), (1, 7)):
-                send(3, qkv_x.at[i], qkv.at[seq, i], g_recv.at[(j * 4 * 2 + 1) * 3 + i], at(dz=dz, core=other))
+        for i in range(3):
+            send(3, qkv_x.at[i], qkv.at[seq, i], g_recv.at[1 * 3 + i], at(dz=1, core=other))
+            g_to_next(seq, 0, i, 0, both=False, down=True)
 
     def g_from_mate():
         for i in range(3):
             arrived(qkv.at[z * 2 + other, i], g_mate.at[i])
         arrived(upb.at[z * 2 + other], u_recv.at[8])
 
+    def below(d, p):
+        return zs[8 - d] * 2 + (c if p == 0 else other)
+
+    def above(d, p):
+        return zs[d] * 2 + (other if p == 0 else c)
+
     def g_hop(d, p):
-        parity = c if p == 0 else other
-        for i in range(3):
-            if d < 4 or p == 0:
-                s = zs[8 - d] * 2 + parity
-                arrived(qkv.at[s, i], g_recv.at[((0 * 4 + d - 1) * 2 + p) * 3 + i])
-                if d < 3 or (d == 3 and p == 0):
-                    g_to_next(s, p, i, d, both=False)
-            if d < 4 or p == 1:
-                s = zs[d] * 2 + parity
-                arrived(qkv.at[s, i], g_recv.at[((1 * 4 + d - 1) * 2 + p) * 3 + i])
-                if d < 3 or (d == 3 and p == 1):
-                    g_to_next(s, p, i, d, both=False, down=True)
+        for i in range(3):
+            s = below(d, p)
+            arrived(qkv.at[s, i], g_recv.at[((0 * 4 + d - 1) * 2 + p) * 3 + i])
+            if d < 3 or (d == 3 and p == 0):
+                g_to_next(s, p, i, d, both=False)
+            s = above(d, p)
+            arrived(qkv.at[s, i], g_recv.at[((1 * 4 + d - 1) * 2 + 1 - p) * 3 + i])
+            if d < 3 or (d == 3 and p == 0):
+                g_to_next(s, 1 - p, i, d, both=False, down=True)
 
     def project():
         for i in range(3):
@@ -180,7 +185,6 @@
     c_own, c_mid, c_end = plane(1, c_unit, 64, c_first, c_rest)
 
     a_own[0]()
-    a_own[1]()
 
     own_ldt.wait()
     total = jnp.concatenate([ldt[...], jnp.zeros((6, 128), F32)], axis=0)
@@ -201,6 +205,7 @@
 
     own_up.wait()
     oth_up.wait()
+    a_own[1]()
     up_own()
     a_mid[0]()
     a_mid[1]()
@@ -234,35 +239,47 @@
     def part(b, i):
         return qkv[b, i]
 
-    def attend(blocks):
+    def prepared(b):
+        parts = upb[b, 128:136].astype(F32)
+        row = parts[0:1] + parts[1:2] + parts[2:3]
+        before = segs[jnp.maximum(b * 128 - 1, 0)]
+        previous = jnp.where(b > 0, before, -1).astype(F32)
+        last = segs[b * 128 + 127].astype(F32)
+        ls_s = jnp.broadcast_to(row, (128, 128))
+        ls_t = ls_s.T
+        seg_s = jnp.broadcast_to(segv[pl.ds(b, 1), :], (128, 128)).astype(F32)
+        seg_t = seg_s.T
+        same = (seg_s == seg_t) & (ti >= si)
+        decay = jnp.where(same, SCALE * jnp.exp(jnp.where(same, ls_t - ls_s, 0.0)), 0.0)
+        ls_last = row[:, 127:128]
+        inflow = jnp.where(seg_t == previous, jnp.exp(ls_t), 0.0)
+        outflow = jnp.where(seg_t == last, jnp.exp(ls_last - ls_t), 0.0)
+        keep = jnp.where(last == previous, jnp.exp(ls_last), 0.0)
+        return decay, inflow, outflow, jnp.broadcast_to(keep, (8, 128))
+
+    def prepare(blocks):
+        for j, b in enumerate(blocks):
+            dec[j], inm[b], outm[b], carry[b] = prepared(b)
+
+    def attend(blocks, ready=False):
         done = []
-        for b in blocks:
-            q, k, v, u = part(b, 0), part(b, 1), part(b, 2), upb[b, 0:128]
-            parts = upb[b, 128:136].astype(F32)
-            row = parts[0:1] + parts[1:2] + parts[2:3]
-            before = segs[jnp.maximum(b * 128 - 1, 0)]
-            previous = jnp.where(b > 0, before, -1).astype(F32)
-            last = segs[b * 128 + 127].astype(F32)
-            ls_s = jnp.broadcast_to(row, (128, 128))
-            ls_t = ls_s.T
-            seg_s = jnp.broadcast_to(segv[pl.ds(b, 1), :], (128, 128)).astype(F32)
-            seg_t = seg_s.T
-            same = (seg_s == seg_t) & (ti >= si)
-            decay = jnp.where(same, SCALE * jnp.exp(jnp.where(same, ls_t - ls_s, 0.0)), 0.0)
-            ls_last = row[:, 127:128]
-            inflow = jnp.where(seg_t == previous, jnp.exp(ls_t), 0.0)
-            outflow = jnp.where(seg_t == last, jnp.exp(ls_last - ls_t), 0.0)
-            keep = jnp.where(last == previous, jnp.exp(ls_last), 0.0)
+        for j, b in enumerate(blocks):
+            q, k, v, u = qkv[b, 0], qkv[b, 1], qkv[b, 2], upb[b, 0:128]
+            if ready:
+                decay, inflow, outflow, keep = dec[j], inm[b], outm[b], None
+            else:
+                decay, inflow, outflow, keep = prepared(b)
             a_qk = (decay * dot(q, k, 1, 1)).astype(BF16)
             a_up = (decay * dot(u, v, 1, 1)).astype(BF16)
             wk_ = (SCALE * outflow * k.astype(F32)).astype(BF16)
             wq_ = (SCALE * inflow * q.astype(F32)).astype(BF16)
             done.append((
-                inflow, outflow, jnp.broadcast_to(keep, (8, 128)), dot(a_up, k, 1, 0), dot(a_up, q, 0, 0),
+                inflow, outflow, keep, dot(a_up, k, 1, 0), dot(a_up, q, 0, 0),
                 dot(a_qk, u, 0, 0), dot(wk_, v, 0, 0), dot(wq_, u, 0, 0),
             ))
         for b, (inflow, outflow, keep, gq, gk, gv, ls, rs) in zip(blocks, done):
-            inm[b], outm[b], carry[b] = inflow, outflow, keep
+            if not ready:
+                inm[b], outm[b], carry[b] = inflow, outflow, keep
             gl[b, 0], gl[b, 1], gl[b, 2] = gq, gk, gv
             lst[b], rst[b] = ls, rs
 
@@ -277,51 +294,60 @@
             view = ct.at[i, :, c]
             send(5, view, view, d_recv.at[i], partner)
 
+    def block(j):
+        return (z * 2 + 10 + j) % 16
+
+    def forward(j, state):
+        b = block(j)
+        inc[b] = state.astype(BF16)
+        return carry[b][0:1] * state + lst[b]
+
+    def backward(i, state):
+        b = block(29 - i)
+        ret[b] = state.astype(BF16)
+        return carry[b][0:1] * state + rst[b]
+
+    def finish(start, count):
+        def run(i, carry_):
+            done = []
+            for b in [block(start + count * i + j) for j in range(count)]:
+                inflow, outflow = inm[b], outm[b]
+                done.append((b, (
+                    gl[b, 0] + inflow * dot(upb[b, 0:128], inc[b], 1, 1),
+                    gl[b, 1] + outflow * dot(qkv[b, 2], ret[b], 1, 1),
+                    gl[b, 2] + outflow * dot(qkv[b, 1], ret[b], 1, 0),
+                )))
+            for b, parts in done:
+                for k, value in enumerate(parts):
+                    grad[b, :, 128 * k : 128 * (k + 1)] = value.astype(BF16)
+            return carry_
+        return run
+
+    last = (zs[4] * 2, zs[4] * 2 + 1)
     attend((seq, z * 2 + other))
-    side = {(1, 0): c_begin, (2, 0): c_mid, (3, 1): c_share}
+    c_begin()
     for d in (1, 2, 3):
         for p in (0, 1):
-            parity = c if p == 0 else other
             g_hop(d, p)
-            attend((zs[8 - d] * 2 + parity, zs[d] * 2 + parity))
+            if (d, p) == (2, 0):
+                c_mid()
+            if (d, p) == (3, 1):
+                c_share()
+            attend((below(d, p), above(d, p)))
             if (d, p) == (1, 1):
                 up_hop(3)
             if (d, p) == (3, 0):
                 up_hop(4)
-            if (d, p) in side:
-                side[d, p]()
-    for p in (0, 1):
-        g_hop(4, p)
-    attend((zs[4] * 2, zs[4] * 2 + 1))
-
-    def forward(b, state):
-        inc[b] = state.astype(BF16)
-        return carry[b][0:1] * state + lst[b]
-
-    lax.fori_loop(0, 16, forward, jnp.zeros((128, 128), F32))
-
-    def backward(i, state):
-        b = 15 - i
-        ret[b] = state.astype(BF16)
-        return carry[b][0:1] * state + rst[b]
-
-    lax.fori_loop(0, 16, backward, jnp.zeros((128, 128), F32))
-
-    def finish(i, carry_):
-        done = []
-        for b in (4 * i, 4 * i + 1, 4 * i + 2, 4 * i + 3):
-            inflow, outflow = inm[b], outm[b]
-            done.append((
-                gl[b, 0] + inflow * dot(upb[b, 0:128], inc[b], 1, 1),
-                gl[b, 1] + outflow * dot(part(b, 2), ret[b], 1, 1),
-                gl[b, 2] + outflow * dot(part(b, 1), ret[b], 1, 0),
-            ))
-        for j, parts in enumerate(done):
-            for k, value in enumerate(parts):
-                grad[4 * i + j, :, 128 * k : 128 * (k + 1)] = value.astype(BF16)
-        return carry_
-
-    lax.fori_loop(0, 4, finish, 0)
+                prepare(last)
+    zero = jnp.zeros((128, 128), F32)
+    state_in = lax.fori_loop(0, 10, forward, zero)
+    state_back = lax.fori_loop(0, 10, backward, zero)
+    finish(4, 6)(0, 0)
+    g_hop(4, 0)
+    attend(last, ready=True)
+    lax.fori_loop(10, 20, forward, state_in)
+    lax.fori_loop(10, 20, backward, state_back)
+    lax.fori_loop(0, 2, finish(10, 5), 0)
     for i in (0, 1):
         arrived(ct.at[i, :, other], d_recv.at[i])
 
@@ -366,6 +392,7 @@
             pltpu.VMEM((16, 128, 128), F32),
             pltpu.VMEM((16, 128, 128), F32),
             pltpu.VMEM((16, 8, 128), F32),
+            pltpu.VMEM((2, 128, 128), F32),
             pltpu.VMEM((16, 128, 128), F32),
             pltpu.VMEM((16, 128, 128), F32),
             pltpu.VMEM((16, 128, 128), BF16),
@@ -382,12 +409,15 @@
             pltpu.SemaphoreType.REGULAR,
         ],
         compiler_params=pltpu.CompilerParams(
-            collective_id=0, has_side_effects=True, vmem_limit_bytes=60 * 1024 * 1024
+            collective_id=0, has_side_effects=True, vmem_limit_bytes=40 * 1024 * 1024
         ),
-    )(
-        tokens, w_query, w_key, w_value, upstream,
-        log_decay.T, segment.reshape(16, 128), segment,
-    )
+    )(*[
+        pltpu.with_memory_space_constraint(a, pltpu.HBM)
+        for a in (
+            tokens, w_query, w_key, w_value, upstream,
+            log_decay.T, segment.reshape(16, 128), segment,
+        )
+    ])
     return out[0], out[1], out[2]
 
 

time: 48 us -> 45.2 us (0.942)
  Pallas kernels: 45.5 us -> 43.7 us
  local copies, waits for them, and re-layouts: 1.78 us -> 0.75 us
    pallas_call x1, Pallas kernels: 45.5 us -> 43.7 us  [local(): pl.pallas_call(kernel, out_shape=jax.ShapeDtypeStruct((3, 256, 256), BF16...]
    squeeze x1, local copies, waits for them, and re-layouts: 1.78 us -> 0.75 us  [local(): return (out[0], out[1], out[2])]
where the time goes in v5:
time: 45.2 us; the launch traced here: 45.1 us
  Pallas kernels  43.7 us (97%)
  local copies, waits for them, and re-layouts  0.75 us (2%)
  between operations  0.64 us (1%)
    pallas_call x1, Pallas kernels, local(): pl.pallas_call(kernel, out_shape=jax.ShapeDtypeStruct((3, 256, 256), BF16...  43.7 us

profile of v5, /device:TPU:1, one launch (start us, length us, event | category | flops | bytes accessed | tf_op | source)
XLA Modules:
  0.0 45.1 jit_solution(12032284860545531631)
XLA Ops:
  0.6 43.7 %shard_map.94 = bf16[3,256,256]{2,1,0:T(8,128)(2,1)S(1)} custom-call(bf16[128,256]{1,0:T(8,128)(2,1)} %tok.1, bf16[4096,256]{1,0:T(8,128)(2,1)} %wq.1, bf16[4096,256]{1,0:T(8,128)(2,1)} %wk.1, bf16[4096,256]{1,0:T(8,128)(2,1)} %wv.1, bf16[128,256]{1,0:T(8,128)(2,1)} %up.1, f32[2,128]{1,0:T(2,128)} %bitcast.9, s32[16,128]{1,0:T(8,128)} %bitcast.8, s32[2048]{0:T(1024)} %segs_in.1), custom_call_target="tpu_custom_call" | custom-call | tf_op jit(solution)/shard_map/pallas_call | solution.py:375
  44.3 0.8 %slice_bitcast_fusion = (bf16[256,256]{1,0:T(8,128)(2,1)}, bf16[256,256]{1,0:T(8,128)(2,1)}, bf16[256,256]{1,0:T(8,128)(2,1)}) fusion(bf16[3,256,256]{2,1,0:T(8,128)(2,1)S(1)} %shard_map.94), kind=kLoop, calls=%fused_computation | loop fusion | bytes 786432 | tf_op jit(solution)/shard_map/squeeze | solution.py:421

commit v6 on v5

--- a/solution.py
+++ b/solution.py
@@ -20,7 +20,7 @@
     tok, wq, wk, wv, up, ldt_in, segv_in, segs_in,
     out,
     ldt, segv, segs, x_all, w_all, qkv, qkv_x, upb, up_x, ct,
-    gl, inm, outm, carry, dec, lst, rst, inc, ret, grad, rows_x, rows_r,
+    gl, inm, outm, carry, dec, lst, rst, inc, ret, grads, rows_a, rows_x, rows_r,
     x_first, x_rest, c_first, c_rest, z_recv, u_recv, g_mate, g_recv, d_recv, o_recv, sends, loc, alive,
 ):
     seq, head = lax.axis_index("seq"), lax.axis_index("head")
@@ -37,7 +37,7 @@
 
     partner = at(core=other)
     barrier = pltpu.get_barrier_semaphore()
-    near = [partner] + [at(dx=i) for i in AROUND] + [at(dy=i) for i in AROUND] + [at(dz=i, core=j) for i in (1, 7) for j in (c, other)]
+    near = [partner] + [at(dx=i) for i in AROUND] + [at(dy=i) for i in AROUND] + [at(dz=i, core=j) for i in (1, 7, 2, 6) for j in (c, other)]
     for dev in near:
         pl.semaphore_signal(barrier, inc=1, device_id=dev, device_id_type=MESH)
 
@@ -59,6 +59,8 @@
 
     own_tok.wait()
     pl.semaphore_wait(barrier, len(near))
+    for i in (1, 7, 2, 6):
+        pl.semaphore_signal(alive, inc=1, device_id=at(dz=i), device_id_type=MESH)
 
     sent = {}
 
@@ -110,49 +112,42 @@
         return own, middle, end
 
     def x_unit(k):
-        return lambda h, half: x_all.at[h, 64 * half + 32 * k : 64 * half + 32 * (k + 1)]
+        return lambda h, half: x_all.at[h, 64 * k + 32 * half : 64 * k + 32 * (half + 1)]
 
     def c_unit(h, half):
         return ct.at[h // 8, 4 * half : 4 * (half + 1), c, h % 8]
 
     def up_own():
         send(2, up_x, upb.at[seq], u_recv.at[8], partner)
-        for i, j in ((1, 0), (7, 4)):
+        for i, j in ((1, 0), (7, 4), (2, 1), (6, 5)):
             send(2, upb.at[seq], upb.at[seq], u_recv.at[j], at(dz=i))
             send(2, up_x, upb.at[seq], u_recv.at[j], at(dz=i, core=other))
 
     def up_hop(d):
-        below, above = zs[8 - d] * 2, zs[d] * 2
+        below_, above_ = zs[8 - d] * 2, zs[d] * 2
         count = 2 if d < 4 else 1
         arrived(upb.at[0:count], u_recv.at[d - 1])
-        if d < 4:
+        if d in (2, 3):
             for parity in (c, other) if d < 3 else (c,):
-                send(2, upb.at[below + parity], upb.at[below + parity], u_recv.at[d], at(dz=1))
+                send(2, upb.at[below_ + parity], upb.at[below_ + parity], u_recv.at[d], at(dz=1))
         arrived(upb.at[0:count], u_recv.at[4 + d - 1])
-        if d < 4:
+        if d in (2, 3):
             for parity in (c, other) if d < 3 else (other,):
-                send(2, upb.at[above + parity], upb.at[above + parity], u_recv.at[4 + d], at(dz=7))
-
-    def g_to_next(s, p, i, d, both=True, down=False):
-        view = qkv.at[s, i]
-        if both or not down:
-            send(3, view, view, g_recv.at[((0 * 4 + d) * 2 + p) * 3 + i], at(dz=1))
-        if both or down:
-            send(3, view, view, g_recv.at[((1 * 4 + d) * 2 + p) * 3 + i], at(dz=7))
-
-    def g_own():
-        for i in range(3):
-            g_to_next(seq, 0, i, 0, both=False)
-            send(3, qkv_x.at[i], qkv.at[seq, i], g_recv.at[(1 * 4 * 2 + 1) * 3 + i], at(dz=7, core=other))
-        for i in range(3):
-            send(3, qkv_x.at[i], qkv.at[seq, i], g_mate.at[i], partner)
-        for i in range(3):
-            send(3, qkv_x.at[i], qkv.at[seq, i], g_recv.at[1 * 3 + i], at(dz=1, core=other))
-            g_to_next(seq, 0, i, 0, both=False, down=True)
+                send(2, upb.at[above_ + parity], upb.at[above_ + parity], u_recv.at[4 + d], at(dz=7))
+
+    def g_send(src, s, k, down, d, p, core):
+        send(3, src, qkv.at[s, k], g_recv.at[((down * 4 + d) * 2 + p) * 2 + k], at(dz=7 if down else 1, core=core))
+
+    def g_own(k):
+        g_send(qkv.at[seq, k], seq, k, 0, 0, 0, c)
+        g_send(qkv_x.at[k], seq, k, 1, 0, 1, other)
+        send(3, qkv_x.at[k], qkv.at[seq, k], g_mate.at[k], partner)
+        g_send(qkv_x.at[k], seq, k, 0, 0, 1, other)
+        g_send(qkv.at[seq, k], seq, k, 1, 0, 0, c)
 
     def g_from_mate():
-        for i in range(3):
-            arrived(qkv.at[z * 2 + other, i], g_mate.at[i])
+        for k in (0, 1):
+            arrived(qkv.at[z * 2 + other, k], g_mate.at[k])
         arrived(upb.at[z * 2 + other], u_recv.at[8])
 
     def below(d, p):
@@ -161,25 +156,20 @@
     def above(d, p):
         return zs[d] * 2 + (other if p == 0 else c)
 
-    def g_hop(d, p):
+    def g_hop(d, p, k):
+        for down, s, q in ((0, below(d, p), p), (1, above(d, p), 1 - p)):
+            arrived(qkv.at[s, k], g_recv.at[((down * 4 + d - 1) * 2 + q) * 2 + k])
+            if d < 3 or (d == 3 and p == 0):
+                g_send(qkv.at[s, k], s, k, down, d, q, c)
+
+    def project(k):
         for i in range(3):
-            s = below(d, p)
-            arrived(qkv.at[s, i], g_recv.at[((0 * 4 + d - 1) * 2 + p) * 3 + i])
-            if d < 3 or (d == 3 and p == 0):
-                g_to_next(s, p, i, d, both=False)
-            s = above(d, p)
-            arrived(qkv.at[s, i], g_recv.at[((1 * 4 + d - 1) * 2 + 1 - p) * 3 + i])
-            if d < 3 or (d == 3 and p == 0):
-                g_to_next(s, 1 - p, i, d, both=False, down=True)
-
-    def project():
-        for i in range(3):
-            acc = dot(x_all[0], w_all[i, 0:256, :], 1, 0)
+            acc = dot(x_all[0, 64 * k : 64 * (k + 1)], w_all[i, 0:256, :], 1, 0)
             for h in range(1, 16):
-                acc = acc + dot(x_all[h], w_all[i, 256 * h : 256 * (h + 1), :], 1, 0)
+                acc = acc + dot(x_all[h, 64 * k : 64 * (k + 1)], w_all[i, 256 * h : 256 * (h + 1), :], 1, 0)
             acc = acc.astype(BF16)
-            qkv[seq, i] = jnp.where(c == 0, acc[:, :128], acc[:, 128:])
-            qkv_x[i] = jnp.where(c == 0, acc[:, 128:], acc[:, :128])
+            qkv[seq, k, i] = jnp.where(c == 0, acc[:, :128], acc[:, 128:])
+            qkv_x[k, i] = jnp.where(c == 0, acc[:, 128:], acc[:, :128])
 
     a_own, a_mid, a_end = zip(*[plane(0, x_unit(k), 32, x_first.at[k], x_rest.at[k]) for k in (0, 1)])
     c_own, c_mid, c_end = plane(1, c_unit, 64, c_first, c_rest)
@@ -210,14 +200,13 @@
     a_mid[0]()
     a_mid[1]()
     up_hop(1)
-    for i in (2, 6):
-        pl.semaphore_signal(alive, inc=1, device_id=at(dz=i), device_id_type=MESH)
+    up_hop(2)
     for copy in weights:
         copy.wait()
     seg_v.wait()
     seg_s.wait()
     a_end[0]()
-    up_hop(2)
+    project(0)
     a_end[1]()
 
     f, group = head // 8, head % 8
@@ -226,18 +215,19 @@
         return x_all.at[2 * zt + f, pl.ds(pl.multiple_of(group * 16, 16), 16)]
 
     own_slice = fetch(slice_of(z), ct.at[f, z, c, group], 0)
-    pl.semaphore_wait(alive, 2)
+    pl.semaphore_wait(alive, 4)
     for i in (4, 3, 5, 2, 6, 1, 7):
         send(4, slice_of(zs[i]), ct.at[f, z, c, group], z_recv.at[0], at(dz=i))
-    project()
-    g_own()
+    g_own(0)
+    project(1)
+    g_own(1)
     g_from_mate()
 
     ti = lax.broadcasted_iota(jnp.int32, (128, 128), 0)
     si = lax.broadcasted_iota(jnp.int32, (128, 128), 1)
 
     def part(b, i):
-        return qkv[b, i]
+        return jnp.concatenate([qkv[b, 0, i], qkv[b, 1, i]], axis=0)
 
     def prepared(b):
         parts = upb[b, 128:136].astype(F32)
@@ -264,7 +254,7 @@
     def attend(blocks, ready=False):
         done = []
         for j, b in enumerate(blocks):
-            q, k, v, u = qkv[b, 0], qkv[b, 1], qkv[b, 2], upb[b, 0:128]
+            q, k, v, u = part(b, 0), part(b, 1), part(b, 2), upb[b, 0:128]
             if ready:
                 decay, inflow, outflow, keep = dec[j], inm[b], outm[b], None
             else:
@@ -314,49 +304,53 @@
                 inflow, outflow = inm[b], outm[b]
                 done.append((b, (
                     gl[b, 0] + inflow * dot(upb[b, 0:128], inc[b], 1, 1),
-                    gl[b, 1] + outflow * dot(qkv[b, 2], ret[b], 1, 1),
-                    gl[b, 2] + outflow * dot(qkv[b, 1], ret[b], 1, 0),
+                    gl[b, 1] + outflow * dot(part(b, 2), ret[b], 1, 1),
+                    gl[b, 2] + outflow * dot(part(b, 1), ret[b], 1, 0),
                 )))
             for b, parts in done:
                 for k, value in enumerate(parts):
-                    grad[b, :, 128 * k : 128 * (k + 1)] = value.astype(BF16)
+                    grads[b // 2, b % 2, :, 128 * k : 128 * (k + 1)] = value.astype(BF16)
             return carry_
         return run
 
     last = (zs[4] * 2, zs[4] * 2 + 1)
     attend((seq, z * 2 + other))
-    c_begin()
+    up_hop(3)
     for d in (1, 2, 3):
-        for p in (0, 1):
-            g_hop(d, p)
-            if (d, p) == (2, 0):
-                c_mid()
-            if (d, p) == (3, 1):
-                c_share()
-            attend((below(d, p), above(d, p)))
-            if (d, p) == (1, 1):
-                up_hop(3)
-            if (d, p) == (3, 0):
-                up_hop(4)
-                prepare(last)
+        g_hop(d, 0, 0)
+        g_hop(d, 1, 0)
+        if d == 1:
+            c_begin()
+        g_hop(d, 0, 1)
+        if d == 2:
+            c_mid()
+        attend((below(d, 0), above(d, 0)))
+        if d == 3:
+            up_hop(4)
+            prepare(last)
+        g_hop(d, 1, 1)
+        attend((below(d, 1), above(d, 1)))
     zero = jnp.zeros((128, 128), F32)
     state_in = lax.fori_loop(0, 10, forward, zero)
     state_back = lax.fori_loop(0, 10, backward, zero)
     finish(4, 6)(0, 0)
-    g_hop(4, 0)
+    c_share()
+    g_hop(4, 0, 0)
+    g_hop(4, 0, 1)
     attend(last, ready=True)
     lax.fori_loop(10, 20, forward, state_in)
     lax.fori_loop(10, 20, backward, state_back)
     lax.fori_loop(0, 2, finish(10, 5), 0)
+    def rows_of(core, parity):
+        right = grads[:, parity].reshape(1024, 384)
+        return dot(ct[core, :, parity].reshape(1024, 256), right, 0, 0)
+
+    rows_a[...] = rows_of(other, c)
     for i in (0, 1):
         arrived(ct.at[i, :, other], d_recv.at[i])
-
-    def rows_of(core):
-        return dot(ct[core].reshape(2048, 256), grad[...].reshape(2048, 384), 0, 0).astype(BF16)
-
-    rows_x[...] = rows_of(other)
+    rows_x[...] = (rows_a[...] + rows_of(other, other)).astype(BF16)
     send(6, rows_x, rows_r, o_recv.at[0], partner)
-    mine = rows_of(c)
+    mine = (rows_of(c, c) + rows_of(c, other)).astype(BF16)
     for i in range(3):
         out[i, :, lanes(c)] = mine[:, 128 * i : 128 * (i + 1)]
     arrived(rows_r, o_recv.at[0])
@@ -383,8 +377,8 @@
             pltpu.SMEM((2048,), jnp.int32),
             pltpu.VMEM((16, 128, 256), BF16),
             pltpu.VMEM((3, 4096, 256), BF16),
-            pltpu.VMEM((16, 3, 128, 128), BF16),
-            pltpu.VMEM((3, 128, 128), BF16),
+            pltpu.VMEM((16, 2, 3, 64, 128), BF16),
+            pltpu.VMEM((2, 3, 64, 128), BF16),
             pltpu.VMEM((16, 136, 128), BF16),
             pltpu.VMEM((136, 128), BF16),
             pltpu.VMEM((2, 8, 2, 8, 16, 256), BF16),
@@ -397,13 +391,14 @@
             pltpu.VMEM((16, 128, 128), F32),
             pltpu.VMEM((16, 128, 128), BF16),
             pltpu.VMEM((16, 128, 128), BF16),
-            pltpu.VMEM((16, 128, 384), BF16),
+            pltpu.VMEM((8, 2, 128, 384), BF16),
+            pltpu.VMEM((256, 384), F32),
             pltpu.VMEM((256, 384), BF16),
             pltpu.VMEM((256, 384), BF16),
             dma((2, 2, 3)), dma((2,)),
             dma((2, 3)), dma(()),
             dma((1,)), dma((9,)),
-            dma((3,)), dma((48,)),
+            dma((2,)), dma((32,)),
             dma((2,)), dma((1,)),
             dma((7,)), dma((10,)),
             pltpu.SemaphoreType.REGULAR,

time: 45.2 us -> 44.1 us (0.976)
  Pallas kernels: 43.7 us -> 42.7 us
    pallas_call x1, Pallas kernels: 43.7 us -> 42.7 us  [local(): pl.pallas_call(kernel, out_shape=jax.ShapeDtypeStruct((3, 256, 256), BF16...]
where the time goes in v6:
time: 44.1 us
  Pallas kernels  42.7 us (97%)
  local copies, waits for them, and re-layouts  0.75 us (2%)
  between operations  0.64 us (1%)
    pallas_call x1, Pallas kernels, local(): pl.pallas_call(kernel, out_shape=jax.ShapeDtypeStruct((3, 256, 256), BF16...  42.7 us

profile of v6, /device:TPU:1, one launch (start us, length us, event | category | flops | bytes accessed | tf_op | source)
XLA Modules:
  0.0 44.1 jit_solution(5399179121026267667)
XLA Ops:
  0.6 42.7 %shard_map.94 = bf16[3,256,256]{2,1,0:T(8,128)(2,1)S(1)} custom-call(bf16[128,256]{1,0:T(8,128)(2,1)} %tok.1, bf16[4096,256]{1,0:T(8,128)(2,1)} %wq.1, bf16[4096,256]{1,0:T(8,128)(2,1)} %wk.1, bf16[4096,256]{1,0:T(8,128)(2,1)} %wv.1, bf16[128,256]{1,0:T(8,128)(2,1)} %up.1, f32[2,128]{1,0:T(2,128)} %bitcast.9, s32[16,128]{1,0:T(8,128)} %bitcast.8, s32[2048]{0:T(1024)} %segs_in.1), custom_call_target="tpu_custom_call" | custom-call | tf_op jit(solution)/shard_map/pallas_call | solution.py:369
  43.3 0.8 %slice_bitcast_fusion = (bf16[256,256]{1,0:T(8,128)(2,1)}, bf16[256,256]{1,0:T(8,128)(2,1)}, bf16[256,256]{1,0:T(8,128)(2,1)}) fusion(bf16[3,256,256]{2,1,0:T(8,128)(2,1)S(1)} %shard_map.94), kind=kLoop, calls=%fused_computation | loop fusion | bytes 786432 | tf_op jit(solution)/shard_map/squeeze | solution.py:416

commit v7 on v6

--- a/solution.py
+++ b/solution.py
@@ -37,7 +37,7 @@
 
     partner = at(core=other)
     barrier = pltpu.get_barrier_semaphore()
-    near = [partner] + [at(dx=i) for i in AROUND] + [at(dy=i) for i in AROUND] + [at(dz=i, core=j) for i in (1, 7, 2, 6) for j in (c, other)]
+    near = [partner] + [at(dx=i) for i in AROUND] + [at(dy=i) for i in AROUND] + [at(dz=i, core=j) for i in (1, 7) for j in (c, other)]
     for dev in near:
         pl.semaphore_signal(barrier, inc=1, device_id=dev, device_id_type=MESH)
 
@@ -55,12 +55,13 @@
     oth_up = fetch(up.at[:, lanes(other)], up_x.at[0:128], 4)
     seg_v = fetch(segv_in, segv, 5)
     seg_s = fetch(segs_in, segs, 6)
-    weights = [fetch(w, w_all.at[i], 7 + i) for i, w in enumerate((wq, wk, wv))]
+    for i, w in enumerate((wq, wk, wv)):
+        fetch(w, w_all.at[i], 7)
 
     own_tok.wait()
     pl.semaphore_wait(barrier, len(near))
-    for i in (1, 7, 2, 6):
-        pl.semaphore_signal(alive, inc=1, device_id=at(dz=i), device_id_type=MESH)
+    for i in (1, 7):
+        pl.semaphore_signal(alive.at[0], inc=1, device_id=at(dz=i), device_id_type=MESH)
 
     sent = {}
 
@@ -84,7 +85,7 @@
     def arrived_rows(rows, recv):
         arrived(w_all.at[0, 0:rows], recv)
 
-    def plane(kind, unit, rows, first, rest):
+    def plane(kind, unit, rows, first, rest, together=False):
         def there(half, stage, d):
             return at(dx=d) if half == stage else at(dy=d)
 
@@ -92,17 +93,20 @@
             for half in (0, 1):
                 for j, d in enumerate(AROUND):
                     view = unit(head, half)
-                    send(kind, view, view, first.at[half, j], there(half, 0, d))
+                    send(kind, view, view, first.at[0] if together else first.at[half, j], there(half, 0, d))
             for half in (0, 1):
                 for d in AROUND:
                     view = unit(head, half)
                     send(kind, view, view, rest, there(half, 1, d))
 
         def middle():
+            if together:
+                arrived_rows(6 * rows, first.at[0])
             for j, d in enumerate(AROUND):
                 for half in (0, 1):
                     view = unit(plane_at(-d, 0) if half == 0 else plane_at(0, -d), half)
-                    arrived(view, first.at[half, j])
+                    if not together:
+                        arrived(view, first.at[half, j])
                     for e in AROUND:
                         send(kind, view, view, rest, there(half, 1, e))
 
@@ -115,11 +119,19 @@
         return lambda h, half: x_all.at[h, 64 * k + 32 * half : 64 * k + 32 * (half + 1)]
 
     def c_unit(h, half):
-        return ct.at[h // 8, 4 * half : 4 * (half + 1), c, h % 8]
+        return ct.at[h // 4, 4 * half : 4 * (half + 1), c, :, h % 4]
 
     def up_own():
         send(2, up_x, upb.at[seq], u_recv.at[8], partner)
-        for i, j in ((1, 0), (7, 4), (2, 1), (6, 5)):
+        for i, j in ((1, 0), (7, 4)):
+            send(2, upb.at[seq], upb.at[seq], u_recv.at[j], at(dz=i))
+            send(2, up_x, upb.at[seq], u_recv.at[j], at(dz=i, core=other))
+
+    def up_two():
+        pl.semaphore_wait(alive.at[0], 2)
+        for i in (2, 6):
+            pl.semaphore_signal(alive.at[1], inc=1, device_id=at(dz=i), device_id_type=MESH)
+        for i, j in ((2, 1), (6, 5)):
             send(2, upb.at[seq], upb.at[seq], u_recv.at[j], at(dz=i))
             send(2, up_x, upb.at[seq], u_recv.at[j], at(dz=i, core=other))
 
@@ -138,10 +150,12 @@
     def g_send(src, s, k, down, d, p, core):
         send(3, src, qkv.at[s, k], g_recv.at[((down * 4 + d) * 2 + p) * 2 + k], at(dz=7 if down else 1, core=core))
 
-    def g_own(k):
+    def g_own_first(k):
         g_send(qkv.at[seq, k], seq, k, 0, 0, 0, c)
         g_send(qkv_x.at[k], seq, k, 1, 0, 1, other)
         send(3, qkv_x.at[k], qkv.at[seq, k], g_mate.at[k], partner)
+
+    def g_own_second(k):
         g_send(qkv_x.at[k], seq, k, 0, 0, 1, other)
         g_send(qkv.at[seq, k], seq, k, 1, 0, 0, c)
 
@@ -171,8 +185,21 @@
             qkv[seq, k, i] = jnp.where(c == 0, acc[:, :128], acc[:, 128:])
             qkv_x[k, i] = jnp.where(c == 0, acc[:, 128:], acc[:, :128])
 
+    quarter, group = head // 4, head % 4
+
+    def slice_of(zt, k):
+        rows = pl.ds(pl.multiple_of(64 * k + 16 * group, 16), 16)
+        return x_all.at[2 * zt + quarter // 2, rows, lanes(quarter % 2)]
+
+    own_slices = []
+
+    def slices_out(k):
+        own_slices.append(fetch(slice_of(z, k), ct.at[quarter, z, c, k, group], k))
+        for i in (4, 3, 5, 2, 6, 1, 7):
+            send(3, slice_of(zs[i], k), ct.at[quarter, z, c, k, group], z_recv.at[0], at(dz=i))
+
     a_own, a_mid, a_end = zip(*[plane(0, x_unit(k), 32, x_first.at[k], x_rest.at[k]) for k in (0, 1)])
-    c_own, c_mid, c_end = plane(1, c_unit, 64, c_first, c_rest)
+    c_own, c_mid, c_end = plane(0, c_unit, 64, c_first, c_rest, together=True)
 
     a_own[0]()
 
@@ -197,30 +224,26 @@
     oth_up.wait()
     a_own[1]()
     up_own()
+    up_two()
     a_mid[0]()
     a_mid[1]()
     up_hop(1)
     up_hop(2)
-    for copy in weights:
-        copy.wait()
+    pltpu.make_async_copy(w_all, w_all, loc.at[7]).wait()
     seg_v.wait()
     seg_s.wait()
     a_end[0]()
+    pl.semaphore_wait(alive.at[1], 2)
+    slices_out(0)
     project(0)
     a_end[1]()
 
-    f, group = head // 8, head % 8
-
-    def slice_of(zt):
-        return x_all.at[2 * zt + f, pl.ds(pl.multiple_of(group * 16, 16), 16)]
-
-    own_slice = fetch(slice_of(z), ct.at[f, z, c, group], 0)
-    pl.semaphore_wait(alive, 4)
-    for i in (4, 3, 5, 2, 6, 1, 7):
-        send(4, slice_of(zs[i]), ct.at[f, z, c, group], z_recv.at[0], at(dz=i))
-    g_own(0)
+    slices_out(1)
+    g_own_first(0)
     project(1)
-    g_own(1)
+    g_own_first(1)
+    g_own_second(0)
+    g_own_second(1)
     g_from_mate()
 
     ti = lax.broadcasted_iota(jnp.int32, (128, 128), 0)
@@ -274,15 +297,16 @@
             lst[b], rst[b] = ls, rs
 
     def c_begin():
-        own_slice.wait()
+        for copy in own_slices:
+            copy.wait()
         arrived_rows(7 * 16, z_recv.at[0])
         c_own()
 
     def c_share():
         c_end()
         for i in (0, 1):
-            view = ct.at[i, :, c]
-            send(5, view, view, d_recv.at[i], partner)
+            view = ct.at[2 * i : 2 * i + 2, :, c]
+            send(1, view, view, d_recv.at[i], partner)
 
     def block(j):
         return (z * 2 + 10 + j) % 16
@@ -318,23 +342,23 @@
     up_hop(3)
     for d in (1, 2, 3):
         g_hop(d, 0, 0)
-        g_hop(d, 1, 0)
+        g_hop(d, 0, 1)
         if d == 1:
             c_begin()
-        g_hop(d, 0, 1)
         if d == 2:
             c_mid()
         attend((below(d, 0), above(d, 0)))
         if d == 3:
             up_hop(4)
             prepare(last)
+        g_hop(d, 1, 0)
         g_hop(d, 1, 1)
         attend((below(d, 1), above(d, 1)))
+    c_share()
     zero = jnp.zeros((128, 128), F32)
     state_in = lax.fori_loop(0, 10, forward, zero)
     state_back = lax.fori_loop(0, 10, backward, zero)
     finish(4, 6)(0, 0)
-    c_share()
     g_hop(4, 0, 0)
     g_hop(4, 0, 1)
     attend(last, ready=True)
@@ -343,13 +367,14 @@
     lax.fori_loop(0, 2, finish(10, 5), 0)
     def rows_of(core, parity):
         right = grads[:, parity].reshape(1024, 384)
-        return dot(ct[core, :, parity].reshape(1024, 256), right, 0, 0)
+        left = jnp.concatenate([ct[2 * core + j, :, parity].reshape(1024, 128) for j in (0, 1)], axis=1)
+        return dot(left, right, 0, 0)
 
     rows_a[...] = rows_of(other, c)
     for i in (0, 1):
-        arrived(ct.at[i, :, other], d_recv.at[i])
+        arrived(ct.at[2 * i : 2 * i + 2, :, other], d_recv.at[i])
     rows_x[...] = (rows_a[...] + rows_of(other, other)).astype(BF16)
-    send(6, rows_x, rows_r, o_recv.at[0], partner)
+    send(3, rows_x, rows_r, o_recv.at[0], partner)
     mine = (rows_of(c, c) + rows_of(c, other)).astype(BF16)
     for i in range(3):
         out[i, :, lanes(c)] = mine[:, 128 * i : 128 * (i + 1)]
@@ -381,7 +406,7 @@
             pltpu.VMEM((2, 3, 64, 128), BF16),
             pltpu.VMEM((16, 136, 128), BF16),
             pltpu.VMEM((136, 128), BF16),
-            pltpu.VMEM((2, 8, 2, 8, 16, 256), BF16),
+            pltpu.VMEM((4, 8, 2, 2, 4, 16, 128), BF16),
             pltpu.VMEM((16, 3, 128, 128), F32),
             pltpu.VMEM((16, 128, 128), F32),
             pltpu.VMEM((16, 128, 128), F32),
@@ -396,12 +421,12 @@
             pltpu.VMEM((256, 384), BF16),
             pltpu.VMEM((256, 384), BF16),
             dma((2, 2, 3)), dma((2,)),
-            dma((2, 3)), dma(()),
+            dma((1,)), dma(()),
             dma((1,)), dma((9,)),
             dma((2,)), dma((32,)),
             dma((2,)), dma((1,)),
-            dma((7,)), dma((10,)),
-            pltpu.SemaphoreType.REGULAR,
+            dma((4,)), dma((8,)),
+            pltpu.SemaphoreType.REGULAR((2,)),
         ],
         compiler_params=pltpu.CompilerParams(
             collective_id=0, has_side_effects=True, vmem_limit_bytes=40 * 1024 * 1024

time: 44.1 us -> 43.5 us (0.986)
  Pallas kernels: 42.7 us -> 42 us
    pallas_call x1, Pallas kernels: 42.7 us -> 42 us  [local(): pl.pallas_call(kernel, out_shape=jax.ShapeDtypeStruct((3, 256, 256), BF16...]
where the time goes in v7:
time: 43.5 us; the launch traced here: 43.4 us
  Pallas kernels  42 us (97%)
  local copies, waits for them, and re-layouts  0.75 us (2%)
  between operations  0.64 us (1%)
    pallas_call x1, Pallas kernels, local(): pl.pallas_call(kernel, out_shape=jax.ShapeDtypeStruct((3, 256, 256), BF16...  42 us

profile of v7, /device:TPU:1, one launch (start us, length us, event | category | flops | bytes accessed | tf_op | source)
XLA Modules:
  0.0 43.4 jit_solution(2404750149778116726)
XLA Ops:
  0.6 42.0 %shard_map.94 = bf16[3,256,256]{2,1,0:T(8,128)(2,1)S(1)} custom-call(bf16[128,256]{1,0:T(8,128)(2,1)} %tok.1, bf16[4096,256]{1,0:T(8,128)(2,1)} %wq.1, bf16[4096,256]{1,0:T(8,128)(2,1)} %wk.1, bf16[4096,256]{1,0:T(8,128)(2,1)} %wv.1, bf16[128,256]{1,0:T(8,128)(2,1)} %up.1, f32[2,128]{1,0:T(2,128)} %bitcast.9, s32[16,128]{1,0:T(8,128)} %bitcast.8, s32[2048]{0:T(1024)} %segs_in.1), custom_call_target="tpu_custom_call" | custom-call | tf_op jit(solution)/shard_map/pallas_call | solution.py:394
  42.7 0.8 %slice_bitcast_fusion = (bf16[256,256]{1,0:T(8,128)(2,1)}, bf16[256,256]{1,0:T(8,128)(2,1)}, bf16[256,256]{1,0:T(8,128)(2,1)}) fusion(bf16[3,256,256]{2,1,0:T(8,128)(2,1)S(1)} %shard_map.94), kind=kLoop, calls=%fused_computation | loop fusion | bytes 786432 | tf_op jit(solution)/shard_map/squeeze | solution.py:441

commit v8 on v7

--- a/solution.py
+++ b/solution.py
@@ -20,7 +20,7 @@
     tok, wq, wk, wv, up, ldt_in, segv_in, segs_in,
     out,
     ldt, segv, segs, x_all, w_all, qkv, qkv_x, upb, up_x, ct,
-    gl, inm, outm, carry, dec, lst, rst, inc, ret, grads, rows_a, rows_x, rows_r,
+    gl, inm, outm, carry, dec, lst, rst, inc, ret, grads, rows_x, rows_r,
     x_first, x_rest, c_first, c_rest, z_recv, u_recv, g_mate, g_recv, d_recv, o_recv, sends, loc, alive,
 ):
     seq, head = lax.axis_index("seq"), lax.axis_index("head")
@@ -228,7 +228,7 @@
     a_mid[0]()
     a_mid[1]()
     up_hop(1)
-    up_hop(2)
+    pl.when(c == 0)(lambda: up_hop(2))
     pltpu.make_async_copy(w_all, w_all, loc.at[7]).wait()
     seg_v.wait()
     seg_s.wait()
@@ -236,10 +236,11 @@
     pl.semaphore_wait(alive.at[1], 2)
     slices_out(0)
     project(0)
+    g_own_first(0)
+    pl.when(c == 1)(lambda: up_hop(2))
     a_end[1]()
 
     slices_out(1)
-    g_own_first(0)
     project(1)
     g_own_first(1)
     g_own_second(0)
@@ -311,15 +312,11 @@
     def block(j):
         return (z * 2 + 10 + j) % 16
 
-    def forward(j, state):
-        b = block(j)
-        inc[b] = state.astype(BF16)
-        return carry[b][0:1] * state + lst[b]
-
-    def backward(i, state):
-        b = block(29 - i)
-        ret[b] = state.astype(BF16)
-        return carry[b][0:1] * state + rst[b]
+    def scan(i, states):
+        ahead, back = states
+        b, e = block(i), block(29 - i)
+        inc[b], ret[e] = ahead.astype(BF16), back.astype(BF16)
+        return carry[b][0:1] * ahead + lst[b], carry[e][0:1] * back + rst[e]
 
     def finish(start, count):
         def run(i, carry_):
@@ -353,29 +350,26 @@
             prepare(last)
         g_hop(d, 1, 0)
         g_hop(d, 1, 1)
+        if d == 3:
+            c_share()
         attend((below(d, 1), above(d, 1)))
-    c_share()
     zero = jnp.zeros((128, 128), F32)
-    state_in = lax.fori_loop(0, 10, forward, zero)
-    state_back = lax.fori_loop(0, 10, backward, zero)
+    states = lax.fori_loop(0, 10, scan, (zero, zero), unroll=5)
     finish(4, 6)(0, 0)
     g_hop(4, 0, 0)
     g_hop(4, 0, 1)
     attend(last, ready=True)
-    lax.fori_loop(10, 20, forward, state_in)
-    lax.fori_loop(10, 20, backward, state_back)
+    lax.fori_loop(10, 20, scan, states, unroll=5)
     lax.fori_loop(0, 2, finish(10, 5), 0)
-    def rows_of(core, parity):
-        right = grads[:, parity].reshape(1024, 384)
-        left = jnp.concatenate([ct[2 * core + j, :, parity].reshape(1024, 128) for j in (0, 1)], axis=1)
-        return dot(left, right, 0, 0)
-
-    rows_a[...] = rows_of(other, c)
+    def rows_of(core):
+        left = jnp.concatenate([ct[2 * core + j].reshape(2048, 128) for j in (0, 1)], axis=1)
+        return dot(left, grads[...].reshape(2048, 384), 0, 0).astype(BF16)
+
     for i in (0, 1):
         arrived(ct.at[2 * i : 2 * i + 2, :, other], d_recv.at[i])
-    rows_x[...] = (rows_a[...] + rows_of(other, other)).astype(BF16)
+    rows_x[...] = rows_of(other)
     send(3, rows_x, rows_r, o_recv.at[0], partner)
-    mine = (rows_of(c, c) + rows_of(c, other)).astype(BF16)
+    mine = rows_of(c)
     for i in range(3):
         out[i, :, lanes(c)] = mine[:, 128 * i : 128 * (i + 1)]
     arrived(rows_r, o_recv.at[0])
@@ -417,7 +411,6 @@
             pltpu.VMEM((16, 128, 128), BF16),
             pltpu.VMEM((16, 128, 128), BF16),
             pltpu.VMEM((8, 2, 128, 384), BF16),
-            pltpu.VMEM((256, 384), F32),
             pltpu.VMEM((256, 384), BF16),
             pltpu.VMEM((256, 384), BF16),
             dma((2, 2, 3)), dma((2,)),

time: 43.5 us -> 43.3 us (level)
  no operation moved by 1% of the time
where the time goes in v8:
time: 43.3 us; the launch traced here: 43.2 us
  Pallas kernels  41.8 us (97%)
  local copies, waits for them, and re-layouts  0.75 us (2%)
  between operations  0.64 us (1%)
    pallas_call x1, Pallas kernels, local(): pl.pallas_call(kernel, out_shape=jax.ShapeDtypeStruct((3, 256, 256), BF16...  41.8 us

profile of v8, /device:TPU:1, one launch (start us, length us, event | category | flops | bytes accessed | tf_op | source)
XLA Modules:
  0.0 43.2 jit_solution(2497516716356917856)
XLA Ops:
  0.6 41.8 %shard_map.94 = bf16[3,256,256]{2,1,0:T(8,128)(2,1)S(1)} custom-call(bf16[128,256]{1,0:T(8,128)(2,1)} %tok.1, bf16[4096,256]{1,0:T(8,128)(2,1)} %wq.1, bf16[4096,256]{1,0:T(8,128)(2,1)} %wk.1, bf16[4096,256]{1,0:T(8,128)(2,1)} %wv.1, bf16[128,256]{1,0:T(8,128)(2,1)} %up.1, f32[2,128]{1,0:T(2,128)} %bitcast.9, s32[16,128]{1,0:T(8,128)} %bitcast.8, s32[2048]{0:T(1024)} %segs_in.1), custom_call_target="tpu_custom_call" | custom-call | tf_op jit(solution)/shard_map/pallas_call | solution.py:388
  42.4 0.8 %slice_bitcast_fusion = (bf16[256,256]{1,0:T(8,128)(2,1)}, bf16[256,256]{1,0:T(8,128)(2,1)}, bf16[256,256]{1,0:T(8,128)(2,1)}) fusion(bf16[3,256,256]{2,1,0:T(8,128)(2,1)S(1)} %shard_map.94), kind=kLoop, calls=%fused_computation | loop fusion | bytes 786432 | tf_op jit(solution)/shard_map/squeeze | solution.py:434

commit v9 on v8

--- a/solution.py
+++ b/solution.py
@@ -360,7 +360,7 @@
     g_hop(4, 0, 1)
     attend(last, ready=True)
     lax.fori_loop(10, 20, scan, states, unroll=5)
-    lax.fori_loop(0, 2, finish(10, 5), 0)
+    finish(10, 10)(0, 0)
     def rows_of(core):
         left = jnp.concatenate([ct[2 * core + j].reshape(2048, 128) for j in (0, 1)], axis=1)
         return dot(left, grads[...].reshape(2048, 384), 0, 0).astype(BF16)

time: 43.3 us -> 43.1 us (level)
  no operation moved by 1% of the time
where the time goes in v9:
time: 43.1 us; the launch traced here: 43 us
  Pallas kernels  41.6 us (97%)
  local copies, waits for them, and re-layouts  0.75 us (2%)
  between operations  0.64 us (1%)
    pallas_call x1, Pallas kernels, local(): pl.pallas_call(kernel, out_shape=jax.ShapeDtypeStruct((3, 256, 256), BF16...  41.6 us

profile of v9, /device:TPU:1, one launch (start us, length us, event | category | flops | bytes accessed | tf_op | source)
XLA Modules:
  0.0 43.0 jit_solution(7605369226089700008)
XLA Ops:
  0.6 41.6 %shard_map.94 = bf16[3,256,256]{2,1,0:T(8,128)(2,1)S(1)} custom-call(bf16[128,256]{1,0:T(8,128)(2,1)} %tok.1, bf16[4096,256]{1,0:T(8,128)(2,1)} %wq.1, bf16[4096,256]{1,0:T(8,128)(2,1)} %wk.1, bf16[4096,256]{1,0:T(8,128)(2,1)} %wv.1, bf16[128,256]{1,0:T(8,128)(2,1)} %up.1, f32[2,128]{1,0:T(2,128)} %bitcast.9, s32[16,128]{1,0:T(8,128)} %bitcast.8, s32[2048]{0:T(1024)} %segs_in.1), custom_call_target="tpu_custom_call" | custom-call | tf_op jit(solution)/shard_map/pallas_call | solution.py:388
  42.3 0.8 %slice_bitcast_fusion = (bf16[256,256]{1,0:T(8,128)(2,1)}, bf16[256,256]{1,0:T(8,128)(2,1)}, bf16[256,256]{1,0:T(8,128)(2,1)}) fusion(bf16[3,256,256]{2,1,0:T(8,128)(2,1)S(1)} %shard_map.94), kind=kLoop, calls=%fused_computation | loop fusion | bytes 786432 | tf_op jit(solution)/shard_map/squeeze | solution.py:434

commit v10 on v9

--- a/solution.py
+++ b/solution.py
@@ -361,20 +361,22 @@
     attend(last, ready=True)
     lax.fori_loop(10, 20, scan, states, unroll=5)
     finish(10, 10)(0, 0)
-    def rows_of(core):
-        left = jnp.concatenate([ct[2 * core + j].reshape(2048, 128) for j in (0, 1)], axis=1)
-        return dot(left, grads[...].reshape(2048, 384), 0, 0).astype(BF16)
+    def rows_of(core, j):
+        return dot(ct[2 * core + j].reshape(2048, 128), grads[...].reshape(2048, 384), 0, 0).astype(BF16)
 
     for i in (0, 1):
         arrived(ct.at[2 * i : 2 * i + 2, :, other], d_recv.at[i])
-    rows_x[...] = rows_of(other)
-    send(3, rows_x, rows_r, o_recv.at[0], partner)
-    mine = rows_of(c)
-    for i in range(3):
-        out[i, :, lanes(c)] = mine[:, 128 * i : 128 * (i + 1)]
-    arrived(rows_r, o_recv.at[0])
-    for i in range(3):
-        out[i, :, lanes(other)] = rows_r[:, 128 * i : 128 * (i + 1)]
+    for j in (0, 1):
+        rows_x[j] = rows_of(other, j)
+        send(3, rows_x.at[j], rows_r.at[j], o_recv.at[j], partner)
+    for j in (0, 1):
+        mine = rows_of(c, j)
+        for i in range(3):
+            out[i, 128 * j : 128 * (j + 1), lanes(c)] = mine[:, 128 * i : 128 * (i + 1)]
+    for j in (0, 1):
+        arrived(rows_r.at[j], o_recv.at[j])
+        for i in range(3):
+            out[i, 128 * j : 128 * (j + 1), lanes(other)] = rows_r[j, :, 128 * i : 128 * (i + 1)]
     for kind, rows in sent.items():
         view = upb.at[0:15] if kind == 2 else w_all.at[0, 0:rows]
         pltpu.make_async_remote_copy(
@@ -411,13 +413,13 @@
             pltpu.VMEM((16, 128, 128), BF16),
             pltpu.VMEM((16, 128, 128), BF16),
             pltpu.VMEM((8, 2, 128, 384), BF16),
-            pltpu.VMEM((256, 384), BF16),
-            pltpu.VMEM((256, 384), BF16),
+            pltpu.VMEM((2, 128, 384), BF16),
+            pltpu.VMEM((2, 128, 384), BF16),
             dma((2, 2, 3)), dma((2,)),
             dma((1,)), dma(()),
             dma((1,)), dma((9,)),
             dma((2,)), dma((32,)),
-            dma((2,)), dma((1,)),
+            dma((2,)), dma((2,)),
             dma((4,)), dma((8,)),
             pltpu.SemaphoreType.REGULAR((2,)),
         ],

time: 43.1 us -> 43.2 us (level)
  no operation moved by 1% of the time
where the time goes in v10:
time: 43.2 us; the launch traced here: 43.1 us
  Pallas kernels  41.7 us (97%)
  local copies, waits for them, and re-layouts  0.75 us (2%)
  between operations  0.64 us (1%)
    pallas_call x1, Pallas kernels, local(): pl.pallas_call(kernel, out_shape=jax.ShapeDtypeStruct((3, 256, 256), BF16...  41.7 us

profile of v10, /device:TPU:1, one launch (start us, length us, event | category | flops | bytes accessed | tf_op | source)
XLA Modules:
  0.0 43.1 jit_solution(13644523017364854707)
XLA Ops:
  0.6 41.7 %shard_map.94 = bf16[3,256,256]{2,1,0:T(8,128)(2,1)S(1)} custom-call(bf16[128,256]{1,0:T(8,128)(2,1)} %tok.1, bf16[4096,256]{1,0:T(8,128)(2,1)} %wq.1, bf16[4096,256]{1,0:T(8,128)(2,1)} %wk.1, bf16[4096,256]{1,0:T(8,128)(2,1)} %wv.1, bf16[128,256]{1,0:T(8,128)(2,1)} %up.1, f32[2,128]{1,0:T(2,128)} %bitcast.9, s32[16,128]{1,0:T(8,128)} %bitcast.8, s32[2048]{0:T(1024)} %segs_in.1), custom_call_target="tpu_custom_call" | custom-call | tf_op jit(solution)/shard_map/pallas_call | solution.py:390
  42.3 0.8 %slice_bitcast_fusion = (bf16[256,256]{1,0:T(8,128)(2,1)}, bf16[256,256]{1,0:T(8,128)(2,1)}, bf16[256,256]{1,0:T(8,128)(2,1)}) fusion(bf16[3,256,256]{2,1,0:T(8,128)(2,1)S(1)} %shard_map.94), kind=kLoop, calls=%fused_computation | loop fusion | bytes 786432 | tf_op jit(solution)/shard_map/squeeze | solution.py:436
